TPU v7x, 32 devices: a whole 2x2x4 slice. The times are simulated.
32 devices in a mesh: gx: 4 (over y, x), gy: 4 (over z), gz: 2 (over core).
Axes of the slice: x: 2, y: 2, z: 4, core: 2. Of those that a mesh axis runs over, the one named last changes fastest.
Arguments:
- provisional: float32 [9, 128, 64, 256], P(None, 'gx', 'gy', 'gz'), may hold values from -6 to 6
- cut_flag: int32 [128, 64, 256], P('gx', 'gy', 'gz'), may hold values from 0 to 1, as said below
- cut_code: int32 [128, 64, 256], P('gx', 'gy', 'gz'), may hold values from 0 to 134217727
- volume_level: int32 [128, 64, 256], P('gx', 'gy', 'gz'), may hold values from 1 to 256
- area_level: int32 [128, 64, 256], P('gx', 'gy', 'gz'), may hold values from 64 to 256
Outputs:
- redistributed: float32 [9, 128, 64, 256], P(None, 'gx', 'gy', 'gz')
- species_change: float32 [9], replicated
Inputs may be any that keep to these rules, and one draw needn't show every extreme that they name: cut_flag marks the cells crossed by one closed embedded surface.
All inputs are finite; a program needn't handle non-finite values.
Results may differ from a plain program's by a relative error of at most 0.00002.
Values sent between devices are 32-bit elements; how exact they have to be, the bound alone decides.
A program may use at most 128 MiB of HBM per device.

v0:
```python
import functools
import math

import jax
import jax.numpy as jnp
from jax import lax
from jax.experimental import pallas as pl
from jax.experimental.pallas import tpu as pltpu
from jax.sharding import PartitionSpec as P

CENTER = 8192
OFFSETS = [(a, b, c) for a in (-1, 0, 1) for b in (-1, 0, 1) for c in (-1, 0, 1)]
AXES = ("gx", "gy", "gz")
MESH = pl.DeviceIdType.MESH
LANES = 128
TILE = 8
GROUP = 16


def kernel(
    nx, ny, scale,
    prov, flag, code, vol, area,
    out, change,
    codes, codes_l, codes_r, carried_a, carried_b, quotas_a, quotas_b, left_a, right_a, left_b, right_b,
    scaling, weights, inverse,
    zs_i, zl_i, zr_i, zs_f, zl_f, zr_f, ys_i, yr_i, ys_f, yr_f, peers,
    send, recv, peer_send, peer_recv,
):
    nspec = prov.shape[0]
    pitch = ny + TILE
    planes = nx + 2
    rows = codes.shape[1]
    tiles = ny // TILE
    here = {axis: lax.axis_index(axis) for axis in AXES}
    size = {axis: lax.axis_size(axis) for axis in AXES}
    lane = lax.broadcasted_iota(jnp.int32, (TILE, LANES), 1)

    barrier = pltpu.get_barrier_semaphore()
    for axis in AXES:
        for k in range(1, size[axis]):
            pl.semaphore_signal(
                barrier, inc=1, device_id={axis: lax.rem(here[axis] + k, size[axis])}, device_id_type=MESH
            )
    pl.semaphore_wait(barrier, sum(size[axis] - 1 for axis in AXES))

    def first(x):
        return TILE + x * pitch

    def own_tile(t):
        row = TILE + (t // tiles + 1) * pitch + lax.rem(t, tiles) * TILE
        return pl.multiple_of(row, TILE), pl.multiple_of(t * TILE, TILE)

    def links(axis, exchange, pairs):
        number = 2 * AXES.index(axis)
        n = size[axis]
        copies = []
        for way, (source, landing) in enumerate(pairs):
            step = 1 if way == 0 else n - 1
            copies.append(
                pltpu.make_async_remote_copy(
                    src_ref=source, dst_ref=landing,
                    send_sem=send.at[exchange, number + way], recv_sem=recv.at[exchange, number + way],
                    device_id={axis: lax.rem(here[axis] + step, n)}, device_id_type=MESH,
                )
            )
        return copies

    def has(axis):
        return here[axis] > 0, here[axis] < size[axis] - 1

    def start(axis, copies):
        below, above = has(axis)
        pl.when(above)(copies[0].start)
        pl.when(below)(copies[1].start)

    def finish(axis, copies):
        below, above = has(axis)
        pl.when(above)(copies[0].wait_send)
        pl.when(below)(copies[0].wait_recv)
        pl.when(below)(copies[1].wait_send)
        pl.when(above)(copies[1].wait_recv)

    def pack(packed, value, field):
        if packed is None:
            packed = jnp.zeros_like(value)
        keep = (lane == 2 * field) | (lane == (2 * field + LANES - 1) % LANES)
        rolled = value if field == 0 else pltpu.roll(value, 2 * field, 1)
        return jnp.where(keep, rolled, packed)

    def exchange(number, buf, zs, zl, zr, ys, yr, fields):
        zero = jnp.zeros((TILE, LANES), buf.dtype)
        z_copies = links("gz", number, ((zs, zl), (zs, zr)))
        start("gz", z_copies)
        yield
        finish("gz", z_copies)
        below, above = has("gz")
        odd = (lane & 1) == 1

        def place(t, carry):
            row, at = own_tile(t)
            low = jnp.where(below, zl[pl.ds(at, TILE), :], zero)
            high = jnp.where(above, zr[pl.ds(at, TILE), :], zero)
            buf[fields, pl.ds(row, TILE), :] = jnp.where(odd, low, high)
            return carry

        lax.fori_loop(0, nx * tiles, place, 0, unroll=4)
        x_copies = links(
            "gx", number,
            (
                (buf.at[:, pl.ds(first(nx), ny), :], buf.at[:, pl.ds(first(0), ny), :]),
                (buf.at[:, pl.ds(first(1), ny), :], buf.at[:, pl.ds(first(nx + 1), ny), :]),
            ),
        )
        start("gx", x_copies)
        yield
        below, above = has("gx")

        def blank(x):
            for field in range(fields + 1):
                buf[field, pl.ds(first(x), ny), :] = jnp.zeros((ny, LANES), buf.dtype)

        pl.when(jnp.logical_not(below))(functools.partial(blank, 0))
        pl.when(jnp.logical_not(above))(functools.partial(blank, nx + 1))
        finish("gx", x_copies)

        chunks = [(x, min(TILE, planes - x)) for x in range(0, planes, TILE)]

        def gather(field, carry):
            for x, count in chunks:
                ys[0, field, pl.ds(x, count), :] = buf[field, pl.ds(first(x) + ny - 1, count, stride=pitch), :]
                ys[1, field, pl.ds(x, count), :] = buf[field, pl.ds(first(x), count, stride=pitch), :]
            return carry

        lax.fori_loop(0, fields + 1, gather, 0)
        y_copies = links("gy", number, ((ys.at[0], yr.at[0]), (ys.at[1], yr.at[1])))
        start("gy", y_copies)
        yield
        finish("gy", y_copies)
        below, above = has("gy")

        def spread(field, carry):
            for x, count in chunks:
                blank_rows = jnp.zeros((count, LANES), buf.dtype)
                low = jnp.where(below, yr[0, field, pl.ds(x, count), :], blank_rows)
                high = jnp.where(above, yr[1, field, pl.ds(x, count), :], blank_rows)
                buf[field, pl.ds(first(x) - 1, count, stride=pitch), :] = low
                buf[field, pl.ds(first(x) + ny, count, stride=pitch), :] = high
            return carry

        lax.fori_loop(0, fields + 1, spread, 0)
        yield

    def shift(buf, to_left, to_right, fields):
        def body(g, carry):
            at = [pl.ds(pl.multiple_of((g * GROUP + k) * TILE, TILE), TILE) for k in range(GROUP)]
            ends = [buf[fields, near, :] for near in at]
            for field in range(fields):
                end = [(pltpu.roll(e, (LANES + 1 - 2 * field) % LANES, 1), pltpu.roll(e, (2 * LANES - 1 - 2 * field) % LANES, 1)) for e in ends]
                for near, e in zip(at, end):
                    value = buf[field, near, :]
                    to_left[field, near, :] = jnp.where(lane == 0, e[0], pltpu.roll(value, 1, 1))
                    to_right[field, near, :] = jnp.where(lane == LANES - 1, e[1], pltpu.roll(value, LANES - 1, 1))
            return carry

        lax.fori_loop(0, rows // (GROUP * TILE), body, 0)

    def fill(t, carry):
        row, at = own_tile(t)
        own = pl.ds(at, TILE)
        value = jnp.where(flag[own, :] == 1, code[own, :] | CENTER, CENTER)
        codes[0, pl.ds(row, TILE), :] = value
        zs_i[own, :] = pack(None, value, 0)
        return carry

    count = nx * tiles

    def loop(body, part=0, parts=1, unroll=4):
        low, high = (count * k // (4 * parts) * 4 for k in (part, part + 1))
        if part == parts - 1:
            high = count
        lax.fori_loop(low, high, body, 0, unroll=unroll)

    cut = nspec // 2
    group_a, group_b = list(range(cut)), list(range(cut, nspec))

    def fractions(own):
        is_cut = flag[own, :] == 1
        volume = jnp.where(is_cut, vol[own, :], 256).astype(jnp.float32) * (1.0 / 256.0)
        face = jnp.where(is_cut, area[own, :], 256).astype(jnp.float32) * (1.0 / 256.0)
        return volume, face

    def peer_copies(axis):
        n = size[axis]
        number = AXES.index(axis)
        return [
            pltpu.make_async_remote_copy(
                src_ref=peers.at[number, here[axis]], dst_ref=peers.at[number, here[axis]],
                send_sem=peer_send.at[number, k], recv_sem=peer_recv.at[number, k],
                device_id={axis: lax.rem(here[axis] + k, n)}, device_id_type=MESH,
            )
            for k in range(1, n)
        ]

    def reduce_start(axis, value):
        peers[AXES.index(axis), here[axis]] = value
        for copy in peer_copies(axis):
            copy.start()

    def reduce_finish(axis):
        number = AXES.index(axis)
        for copy in peer_copies(axis):
            copy.wait()
        value = peers[number, 0]
        for k in range(1, size[axis]):
            value = value + peers[number, k]
        return value

    loop(fill, unroll=4)
    code_steps = exchange(0, codes, zs_i, zl_i, zr_i, ys_i, yr_i, 1)
    next(code_steps)

    def add_up(t, totals):
        _, at = own_tile(t)
        own = pl.ds(at, TILE)
        volume, _ = fractions(own)
        return tuple(totals[s] + volume * prov[s, own, :] for s in range(nspec))

    def add_part(part, totals):
        low, high = (count * k // 12 * 4 for k in (part, part + 1))
        return lax.fori_loop(low, high if part < 2 else count, add_up, totals, unroll=4)

    totals = tuple(jnp.zeros((TILE, LANES), jnp.float32) for _ in range(nspec))
    for part in range(3):
        totals = add_part(part, totals)
        next(code_steps)
    local = jnp.concatenate(
        [jnp.sum(total, axis=0, keepdims=True) for total in totals]
        + [jnp.zeros((peers.shape[2] - nspec, LANES), jnp.float32)],
        axis=0,
    )
    reduce_start("gx", local)
    shift(codes, codes_l, codes_r, 1)
    code_at = {-1: codes_l, 0: codes, 1: codes_r}

    def weigh_a(t, carry):
        row, at = own_tile(t)
        own = pl.ds(at, TILE)
        counted = jnp.zeros((TILE, LANES), jnp.int32)
        for position, (a, b, c) in enumerate(OFFSETS):
            near = code_at[-c][0, pl.ds(row - a * pitch - b, TILE), :]
            counted = counted + (lax.shift_right_logical(near, position) & 1)
        volume, face = fractions(own)
        share = 1.0 / counted.astype(jnp.float32)
        scaling[own, :] = face * share
        weight = volume * share
        weights[own, :] = weight
        packed = None
        for f, s in enumerate(group_a):
            value = weight * prov[s, own, :]
            carried_a[f, pl.ds(row, TILE), :] = value
            packed = pack(packed, value, f)
        value = weight * face
        carried_a[cut, pl.ds(row, TILE), :] = value
        zs_f[0, own, :] = pack(packed, value, cut)
        return carry

    def weigh_b(t, carry):
        row, at = own_tile(t)
        own = pl.ds(at, TILE)
        weight = weights[own, :]
        packed = None
        for f, s in enumerate(group_b):
            value = weight * prov[s, own, :]
            carried_b[f, pl.ds(row, TILE), :] = value
            packed = pack(packed, value, f)
        zs_f[1, own, :] = packed
        return carry

    def exchange_f(number, buf, fields):
        k = number - 1
        return exchange(
            number, buf, zs_f.at[k], zl_f.at[k], zr_f.at[k],
            ys_f.at[k, :, pl.ds(0, fields + 1)], yr_f.at[k, :, pl.ds(0, fields + 1)], fields,
        )

    def taps(t, fields, at_shift, sign):
        row, _ = own_tile(t)
        zero = jnp.zeros((TILE, LANES), jnp.float32)
        found = [zero] * fields
        mine = codes[0, pl.ds(row, TILE), :] if sign > 0 else None
        for position, (a, b, c) in enumerate(OFFSETS):
            near = pl.ds(row + sign * (a * pitch + b), TILE)
            code_here = mine if sign > 0 else code_at[-c][0, near, :]
            present = (code_here & (1 << position)) != 0
            for f in range(fields):
                found[f] = found[f] + jnp.where(present, at_shift[sign * c][f, near, :], zero)
        return found

    def quota_a(t, carry):
        row, at = own_tile(t)
        found = taps(t, cut + 1, {-1: left_a, 0: carried_a, 1: right_a}, 1)
        inverted = 1.0 / found[cut]
        inverse[pl.ds(at, TILE), :] = inverted
        packed = None
        for f in range(cut):
            value = found[f] * inverted
            quotas_a[f, pl.ds(row, TILE), :] = value
            packed = pack(packed, value, f)
        zs_f[2, pl.ds(at, TILE), :] = packed
        return carry

    def quota_b(t, carry):
        row, at = own_tile(t)
        found = taps(t, len(group_b), {-1: left_b, 0: carried_b, 1: right_b}, 1)
        inverted = inverse[pl.ds(at, TILE), :]
        packed = None
        for f in range(len(group_b)):
            value = found[f] * inverted
            quotas_b[f, pl.ds(row, TILE), :] = value
            packed = pack(packed, value, f)
        zs_f[3, pl.ds(at, TILE), :] = packed
        return carry

    def scatter(group, buf, left, right, t, carry):
        _, at = own_tile(t)
        own = pl.ds(at, TILE)
        found = taps(t, len(group), {-1: left, 0: buf, 1: right}, -1)
        factor = scaling[own, :]
        for f, s in enumerate(group):
            out[s, own, :] = factor * found[f]
        return carry

    scatter_a = functools.partial(scatter, group_a, quotas_a, left_a, right_a)
    scatter_b = functools.partial(scatter, group_b, quotas_b, left_b, right_b)

    loop(weigh_a)
    steps_a = exchange_f(1, carried_a, cut + 1)
    next(steps_a)
    loop(weigh_b)
    steps_b = exchange_f(2, carried_b, len(group_b))
    next(steps_b)
    next(steps_a)
    next(steps_b)
    reduce_start("gy", reduce_finish("gx"))
    next(steps_a)
    next(steps_b)
    next(steps_a)
    shift(carried_a, left_a, right_a, cut + 1)
    loop(quota_a)
    steps_qa = exchange_f(3, quotas_a, cut)
    next(steps_qa)
    next(steps_b)
    shift(carried_b, left_b, right_b, len(group_b))
    next(steps_qa)
    loop(quota_b, 0, 2)
    next(steps_qa)
    loop(quota_b, 1, 2)
    steps_qb = exchange_f(4, quotas_b, len(group_b))
    next(steps_qb)
    reduce_start("gz", reduce_finish("gy"))
    next(steps_qa)
    next(steps_qb)
    shift(quotas_a, left_a, right_a, cut)
    next(steps_qb)
    loop(scatter_a)
    summed = reduce_finish("gz")
    change[...] = jnp.broadcast_to(jnp.sum(summed, axis=1, keepdims=True) * scale, change.shape)
    next(steps_qb)
    shift(quotas_b, left_b, right_b, len(group_b))
    loop(scatter_b)


def per_device(provisional, cut_flag, cut_code, volume_level, area_level):
    nspec, nx, ny, nz = provisional.shape
    assert nz == LANES and ny % TILE == 0
    own = nx * ny
    planes = nx + 2
    rows = -(-(TILE + planes * (ny + TILE)) // (GROUP * TILE)) * (GROUP * TILE)
    slab = -(-planes // TILE) * TILE
    most = max(lax.axis_size(axis) for axis in AXES)
    cells = own * nz * math.prod(lax.axis_size(axis) for axis in AXES)
    high = -(-nspec // TILE) * TILE
    cut = nspec // 2
    rest = nspec - cut
    f32, i32 = jnp.float32, jnp.int32
    vmem = pl.BlockSpec(memory_space=pltpu.VMEM)
    shapes = [
        ((2, rows, nz), i32), ((1, rows, nz), i32), ((1, rows, nz), i32),
        ((cut + 2, rows, nz), f32), ((rest + 1, rows, nz), f32),
        ((cut + 1, rows, nz), f32), ((rest + 1, rows, nz), f32),
        ((cut + 1, rows, nz), f32), ((cut + 1, rows, nz), f32),
        ((rest, rows, nz), f32), ((rest, rows, nz), f32),
        ((own, nz), f32), ((own, nz), f32), ((own, nz), f32),
        ((own, nz), i32), ((own, nz), i32), ((own, nz), i32),
        ((4, own, nz), f32), ((4, own, nz), f32), ((4, own, nz), f32),
        ((2, 2, slab, nz), i32), ((2, 2, slab, nz), i32),
        ((4, 2, rest + 1, slab, nz), f32), ((4, 2, rest + 1, slab, nz), f32),
        ((3, most, high, nz), f32),
    ]
    out, change = pl.pallas_call(
        functools.partial(kernel, nx, ny, 1.0 / math.sqrt(cells)),
        out_shape=(
            jax.ShapeDtypeStruct((nspec, own, nz), f32),
            jax.ShapeDtypeStruct((high, nz), f32),
        ),
        in_specs=[vmem] * 5,
        out_specs=(vmem, vmem),
        scratch_shapes=[pltpu.VMEM(shape, kind) for shape, kind in shapes]
        + [
            pltpu.SemaphoreType.DMA((5, 6)), pltpu.SemaphoreType.DMA((5, 6)),
            pltpu.SemaphoreType.DMA((3, most)), pltpu.SemaphoreType.DMA((3, most)),
        ],
        compiler_params=pltpu.CompilerParams(
            collective_id=0, has_side_effects=True, vmem_limit_bytes=60 * 1024 * 1024
        ),
    )(
        provisional.reshape(nspec, own, nz),
        cut_flag.reshape(own, nz),
        cut_code.reshape(own, nz),
        volume_level.reshape(own, nz),
        area_level.reshape(own, nz),
    )
    return out.reshape(provisional.shape), change[:nspec, 0]


def solution(mesh):
    spec = P("gx", "gy", "gz")
    wide = P(None, "gx", "gy", "gz")
    return jax.shard_map(
        per_device, mesh=mesh, in_specs=(wide, spec, spec, spec, spec), out_specs=(wide, P()), check_vma=False
    )
```

profile of v0, /device:TPU:0, one launch (start us, length us, event | category | flops | bytes accessed | tf_op | source)
XLA Modules:
  0.0 70.6 jit_solution(7148432798001816566)
XLA Ops:
  0.6 65.4 %shard_map.68 = (f32[9,512,128]{2,1,0:T(8,128)}, f32[16,128]{1,0:T(8,128)}) custom-call(f32[9,512,128]{2,1,0:T(8,128)} %bitcast.7, s32[512,128]{1,0:T(8,128)} %bitcast.8, s32[512,128]{1,0:T(8,128)} %bitcast.9, s32[512,128]{1,0:T(8,128)} %bitcast.10, s32[512,128]{1,0:T(8,128)} %bitcast.11), custom_call_target="tpu_custom_call" | custom-call | tf_op jit(solution)/shard_map/pallas_call | solution.py:400
  66.1 1.3 %slice_reduce_fusion = f32[9]{0:T(128)} fusion(f32[16,128]{1,0:T(8,128)} %get-tuple-element.5), kind=kLoop, calls=%fused_computation | loop fusion | bytes 72 | tf_op jit(solution)/shard_map/slice | solution.py:423
  67.4 3.2 %copy.8 = f32[9,32,16,128]{3,2,1,0:T(8,128)} copy(f32[9,32,16,128]{3,2,1,0:T(8,128)} %bitcast.6) | data formatting | bytes 4718592
where the time goes:
time: 70.8 us; the launch traced here: 70.6 us
  Pallas kernels  65.4 us (92%)
  local copies, waits for them, and re-layouts  4.54 us (6%)
    pallas_call x1, Pallas kernels, per_device(): pl.pallas_call(functools.partial(kernel, nx, ny, 1.0 / math.sqrt(cells)),...  65.4 us
    unnamed x1, local copies, waits for them, and re-layouts  3.22 us

commit v1 on v0

v1 whole, which is shorter than its diff:
```python
import functools
import math

import jax
import jax.numpy as jnp
from jax import lax
from jax.experimental import pallas as pl
from jax.experimental.pallas import tpu as pltpu
from jax.sharding import PartitionSpec as P

CENTER = 8192
BLOCK = [(a, b, 9 * (a + 1) + 3 * (b + 1)) for a in (-1, 0, 1) for b in (-1, 0, 1)]
AXES = ("gx", "gy", "gz")
WAYS = [(1, 0), (-1, 0), (0, 1), (0, -1), (1, 1), (1, -1), (-1, 1), (-1, -1)]
MESH = pl.DeviceIdType.MESH
LANES = 128
TILE = 8


def pipelined(stages, count, hook=None):
    depth = len(stages)

    def step(i, lowest, highest):
        for k in reversed(range(lowest, highest)):
            stages[k](i - k)

    for i in range(min(depth - 1, count)):
        step(i, 0, i + 1)

    def body(i, carry):
        if hook is not None:
            at, action = hook
            pl.when(i == at)(action)
        step(i, 0, depth)
        return carry

    lax.fori_loop(depth - 1, count, body, 0)
    for i in range(count, count + depth - 1):
        step(i, i - count + 1, depth)


def kernel(
    nx, ny, scale,
    prov_h, flag_h, code_h, vol_h, area_h,
    out_h, change,
    prov, flag, code, vol, area, out,
    codes, wbuf, qbuf, shifted, edge,
    zs_i, zl_i, zr_i, zs_f, zl_f, zr_f,
    ys_i, yr_i, cs_i, cr_i, ys_w, yr_w, cs_w, cr_w, ys_q, yr_q, cs_q, cr_q,
    weights, scaling, ends, parts_i, parts_f, peers,
    load, store, z_send, z_recv, send, recv, peer_send, peer_recv,
):
    nspec = prov.shape[0]
    pitch = ny + TILE
    tiles = ny // TILE
    count = nx * tiles
    here = {axis: lax.axis_index(axis) for axis in AXES}
    size = {axis: lax.axis_size(axis) for axis in AXES}
    lane = lax.broadcasted_iota(jnp.int32, (TILE, LANES), 1)
    odd = (lane & 1) == 1
    first_lane = lane == 0
    last_lane = lane == LANES - 1
    both_ends = first_lane | last_lane
    cut = nspec // 2
    flux = cut
    fields = nspec + 1
    group_a, group_b = list(range(cut)), list(range(cut, nspec))

    inputs = [(flag_h, flag), (code_h, code), (vol_h, vol), (area_h, area), (prov_h, prov)]
    loads = [pltpu.make_async_copy(src, dst, load.at[k]) for k, (src, dst) in enumerate(inputs)]
    for copy in loads:
        copy.start()

    def moved(axis, step):
        return lax.rem(here[axis] + (step + size[axis]), size[axis])

    barrier = pltpu.get_barrier_semaphore()
    others = set()
    for dx, dy in WAYS:
        others.add((dx % size["gx"], dy % size["gy"], 0))
    for number, axis in enumerate(AXES):
        for k in range(1, size[axis]):
            others.add(tuple(k if i == number else 0 for i in range(3)))
    others.discard((0, 0, 0))
    for shift in sorted(others):
        pl.semaphore_signal(
            barrier, inc=1,
            device_id={axis: lax.rem(here[axis] + shift[i], size[axis]) for i, axis in enumerate(AXES)},
            device_id_type=MESH,
        )

    def first(x):
        return TILE + x * pitch

    def own_tile(t):
        row = TILE + (t // tiles + 1) * pitch + lax.rem(t, tiles) * TILE
        return pl.multiple_of(row, TILE), pl.multiple_of(t * TILE, TILE)

    def side(axis, step):
        return here[axis] < size[axis] - 1 if step > 0 else here[axis] > 0

    def exists(dx, dy):
        found = None
        for axis, step in (("gx", dx), ("gy", dy)):
            if step:
                there = side(axis, step)
                found = there if found is None else jnp.logical_and(found, there)
        return found

    below_z, above_z = side("gz", -1), side("gz", 1)

    def edge_row(step):
        return ny - 1 if step > 0 else 0

    def halo_row(step):
        return ny if step > 0 else -1

    def blank(buf, low, high):
        zeros = jnp.zeros((ny, LANES), buf.dtype)
        row_zeros = jnp.zeros((TILE, LANES), buf.dtype)
        one = jnp.zeros((1, LANES), buf.dtype)

        def plane(step):
            def body(f, carry):
                buf[f, pl.ds(first(nx + 1 if step > 0 else 0), ny), :] = zeros
                return carry
            lax.fori_loop(low, high, body, 0)

        def row(step):
            def body(f, carry):
                for x in range(0, nx, TILE):
                    buf[f, pl.ds(first(x + 1) + halo_row(step), TILE, stride=pitch), :] = row_zeros
                return carry
            lax.fori_loop(low, high, body, 0)

        def corner(dx, dy):
            def body(f, carry):
                buf[f, pl.ds(first(nx + 1 if dx > 0 else 0) + halo_row(dy), 1), :] = one
                return carry
            lax.fori_loop(low, high, body, 0)

        for dx, dy in WAYS:
            action = functools.partial(plane, dx) if dy == 0 else (
                functools.partial(row, dy) if dx == 0 else functools.partial(corner, dx, dy))
            pl.when(jnp.logical_not(exists(dx, dy)))(action)

    class Unit:
        def __init__(self, number, buf, low, high, ys, yr, cs, cr, corner):
            self.buf, self.low, self.high = buf, low, high
            self.ys, self.yr, self.cs, self.cr, self.corner = ys, yr, cs, cr, corner
            n = high - low
            ends_of = {1: (nx, 0), -1: (1, nx + 1)}
            self.copies = []
            for k, (dx, dy) in enumerate(WAYS):
                if dy == 0:
                    here_x, there_x = ends_of[dx]
                    source = buf.at[pl.ds(low, n), pl.ds(first(here_x), ny), :]
                    landing = buf.at[pl.ds(low, n), pl.ds(first(there_x), ny), :]
                elif dx == 0:
                    way = 0 if dy > 0 else 1
                    source, landing = ys.at[way, pl.ds(low, n)], yr.at[way, pl.ds(low, n)]
                else:
                    source, landing = cs.at[corner, k - 4], cr.at[corner, k - 4]
                self.copies.append(
                    pltpu.make_async_remote_copy(
                        src_ref=source, dst_ref=landing,
                        send_sem=send.at[number, k], recv_sem=recv.at[number, k],
                        device_id={"gx": moved("gx", dx), "gy": moved("gy", dy)}, device_id_type=MESH,
                    )
                )

        def start(self):
            buf = self.buf
            for k, (dx, dy) in enumerate(WAYS):
                if dy == 0:
                    pl.when(exists(dx, dy))(self.copies[k].start)

            def gather(f, carry):
                for x in range(0, nx, TILE):
                    for way, step in ((0, 1), (1, -1)):
                        self.ys[way, f, pl.ds(x, TILE), :] = buf[f, pl.ds(first(x + 1) + edge_row(step), TILE, stride=pitch), :]
                for k, (dx, dy) in enumerate(WAYS[4:]):
                    row = first(nx if dx > 0 else 1) + edge_row(dy)
                    self.cs[self.corner, k, pl.ds(f - self.low, 1), :] = buf[f, pl.ds(row, 1), :]
                return carry

            lax.fori_loop(self.low, self.high, gather, 0)
            for k, (dx, dy) in enumerate(WAYS):
                if dy != 0:
                    pl.when(exists(dx, dy))(self.copies[k].start)

        def receive(self):
            buf = self.buf
            for k, (dx, dy) in enumerate(WAYS):
                pl.when(exists(-dx, -dy))(self.copies[k].wait_recv)

            def rows(way, step):
                def body(f, carry):
                    for x in range(0, nx, TILE):
                        buf[f, pl.ds(first(x + 1) + halo_row(-step), TILE, stride=pitch), :] = self.yr[way, f, pl.ds(x, TILE), :]
                    return carry
                lax.fori_loop(self.low, self.high, body, 0)

            def corner(k, dx, dy):
                def body(f, carry):
                    row = first(0 if dx > 0 else nx + 1) + halo_row(-dy)
                    buf[f, pl.ds(row, 1), :] = self.cr[self.corner, k, pl.ds(f - self.low, 1), :]
                    return carry
                lax.fori_loop(self.low, self.high, body, 0)

            for way, step in ((0, 1), (1, -1)):
                pl.when(exists(0, -step))(functools.partial(rows, way, step))
            for k, (dx, dy) in enumerate(WAYS[4:]):
                pl.when(exists(-dx, -dy))(functools.partial(corner, k, dx, dy))

        def finish(self):
            for k, (dx, dy) in enumerate(WAYS):
                pl.when(exists(dx, dy))(self.copies[k].wait_send)

    class Depth:
        def __init__(self, number, zs, zl, zr, buf, plane):
            self.zl, self.zr, self.buf, self.plane = zl, zr, buf, plane
            self.copies = [
                pltpu.make_async_remote_copy(
                    src_ref=zs, dst_ref=landing,
                    send_sem=z_send.at[number, way], recv_sem=z_recv.at[number, way],
                    device_id={"gz": moved("gz", step)}, device_id_type=MESH,
                )
                for way, (landing, step) in enumerate(((zl, 1), (zr, -1)))
            ]

        def start(self):
            pl.when(above_z)(self.copies[0].start)
            pl.when(below_z)(self.copies[1].start)

        def receive(self):
            pl.when(below_z)(self.copies[0].wait_recv)
            pl.when(above_z)(self.copies[1].wait_recv)
            zero = jnp.zeros((TILE, LANES), self.buf.dtype)

            def place(t, carry):
                row, at = own_tile(t)
                low = jnp.where(below_z, self.zl[pl.ds(at, TILE), :], zero)
                high = jnp.where(above_z, self.zr[pl.ds(at, TILE), :], zero)
                self.buf[self.plane, pl.ds(row, TILE), :] = jnp.where(odd, low, high)
                return carry

            lax.fori_loop(0, count, place, 0, unroll=8)

        def finish(self):
            pl.when(above_z)(self.copies[0].wait_send)
            pl.when(below_z)(self.copies[1].wait_send)

    code_z = Depth(0, zs_i, zl_i, zr_i, codes, 1)
    code_own = Unit(0, codes, 0, 1, ys_i, yr_i, cs_i, cr_i, 0)
    code_packed = Unit(1, codes, 1, 2, ys_i, yr_i, cs_i, cr_i, 1)
    w_z = Depth(1, zs_f.at[0], zl_f.at[0], zr_f.at[0], wbuf, fields)
    w_a = Unit(2, wbuf, 0, cut + 1, ys_w, yr_w, cs_w, cr_w, 0)
    w_b = Unit(3, wbuf, cut + 1, fields, ys_w, yr_w, cs_w, cr_w, 1)
    w_packed = Unit(4, wbuf, fields, fields + 1, ys_w, yr_w, cs_w, cr_w, 2)
    qa_z = Depth(2, zs_f.at[1], zl_f.at[1], zr_f.at[1], qbuf, nspec)
    q_a = Unit(5, qbuf, 0, cut, ys_q, yr_q, cs_q, cr_q, 0)
    qa_packed = Unit(6, qbuf, nspec, nspec + 1, ys_q, yr_q, cs_q, cr_q, 1)
    qb_z = Depth(3, zs_f.at[2], zl_f.at[2], zr_f.at[2], qbuf, nspec + 1)
    q_b = Unit(7, qbuf, cut, nspec, ys_q, yr_q, cs_q, cr_q, 2)
    qb_packed = Unit(8, qbuf, nspec + 1, nspec + 2, ys_q, yr_q, cs_q, cr_q, 3)
    everything = [code_z, code_own, code_packed, w_z, w_a, w_b, w_packed, qa_z, q_a, qa_packed, qb_z, q_b, qb_packed]

    def peer_copies(axis):
        number = AXES.index(axis)
        return [
            pltpu.make_async_remote_copy(
                src_ref=peers.at[number, here[axis]], dst_ref=peers.at[number, here[axis]],
                send_sem=peer_send.at[number, k], recv_sem=peer_recv.at[number, k],
                device_id={axis: lax.rem(here[axis] + k, size[axis])}, device_id_type=MESH,
            )
            for k in range(1, size[axis])
        ]

    def reduce_start(axis, value):
        peers[AXES.index(axis), here[axis]] = value
        for copy in peer_copies(axis):
            copy.start()

    def reduce_finish(axis):
        number = AXES.index(axis)
        for copy in peer_copies(axis):
            copy.wait()
        value = peers[number, 0]
        for k in range(1, size[axis]):
            value = value + peers[number, k]
        return value

    def fractions(own):
        is_cut = flag[own, :] == 1
        volume = jnp.where(is_cut, vol[own, :], 256).astype(jnp.float32) * (1.0 / 256.0)
        face = jnp.where(is_cut, area[own, :], 256).astype(jnp.float32) * (1.0 / 256.0)
        return volume, face

    def fill(t, carry):
        row, at = own_tile(t)
        own = pl.ds(at, TILE)
        value = jnp.where(flag[own, :] == 1, code[own, :] | CENTER, CENTER)
        codes[0, pl.ds(row, TILE), :] = value
        shifted[0, own, :] = jnp.where(first_lane, 0, pltpu.roll(value, 1, 1))
        shifted[1, own, :] = jnp.where(last_lane, 0, pltpu.roll(value, LANES - 1, 1))
        low = jnp.broadcast_to(value[:, :1], (TILE, LANES))
        high = lax.shift_right_logical(jnp.broadcast_to(value[:, LANES - 1:], (TILE, LANES)), 2)
        zs_i[own, :] = jnp.where(odd, high, low)
        edge[own, :] = jnp.where(odd, low, high)
        return carry

    def add_up(t, totals):
        _, at = own_tile(t)
        own = pl.ds(at, TILE)
        volume, _ = fractions(own)
        return tuple(totals[s] + volume * prov[s, own, :] for s in range(nspec))

    def taps(row, step, left, middle, right, buf, low, high):
        zero = jnp.zeros((TILE, LANES), jnp.float32)
        sums = [[None] * (high - low) for _ in range(3)]
        for a, b, position in BLOCK:
            near = pl.ds(row + step * (a * pitch + b), TILE)
            present = []
            for k, source in enumerate((left, middle, right)):
                if step > 0 and position + k == 13:
                    present.append(None)
                else:
                    present.append((source(near) & (1 << (position + k))) != 0)
            for f in range(low, high):
                value = buf[f, near, :]
                for k in range(3):
                    term = value if present[k] is None else jnp.where(present[k], value, zero)
                    old = sums[k][f - low]
                    sums[k][f - low] = term if old is None else old + term
        return sums

    def packed_taps(row, step, source, buf, plane):
        zero = jnp.zeros((TILE, LANES), jnp.float32)
        total = None
        for a, b, position in BLOCK:
            near = pl.ds(row + step * (a * pitch + b), TILE)
            term = jnp.where((source(near) & (1 << position)) != 0, buf[plane, near, :], zero)
            total = term if total is None else total + term
        return total

    def pack(values, lowest):
        packed = jnp.zeros((TILE, LANES), jnp.float32)
        for k, value in enumerate(values):
            f = lowest + k
            start = value if f == 0 else pltpu.roll(value, 2 * f, 1)
            packed = jnp.where(lane == 2 * f, start, packed)
            packed = jnp.where(lane == 2 * f + 1, pltpu.roll(value, 2 * f + 2, 1), packed)
        return packed

    quad = 4

    def count_taps(g):
        for k in range(quad):
            row, at = own_tile(g * quad + k)
            sums = [None] * 3
            total = None
            for a, b, position in BLOCK:
                near = pl.ds(row - a * pitch - b, TILE)
                value = codes[0, near, :]
                value = value if position == 0 else lax.shift_right_logical(value, position)
                for m in range(3):
                    term = value & (1 << m)
                    sums[m] = term if sums[m] is None else sums[m] + term
                value = codes[1, near, :]
                value = value if position == 0 else lax.shift_right_logical(value, position)
                total = value & 1 if total is None else total + (value & 1)
            for m in range(3):
                parts_i[k, m] = sums[m]
            parts_i[k, 3] = total

    def weigh(g):
        for k in range(quad):
            row, at = own_tile(g * quad + k)
            own = pl.ds(at, TILE)
            from_end = pltpu.roll(parts_i[k, 3], LANES - 1, 1)
            from_left = pltpu.roll(lax.shift_right_logical(parts_i[k, 2], 2), 1, 1)
            from_right = pltpu.roll(parts_i[k, 0], LANES - 1, 1)
            counted = lax.shift_right_logical(parts_i[k, 1], 1)
            counted = counted + jnp.where(first_lane, from_end, from_left) + jnp.where(last_lane, from_end, from_right)
            volume, face = fractions(own)
            share = 1.0 / counted.astype(jnp.float32)
            scaling[own, :] = face * share
            weight = volume * share
            for s in range(nspec):
                f = s if s < cut else s + 1
                wbuf[f, pl.ds(row, TILE), :] = weight * prov[s, own, :]
            wbuf[flux, pl.ds(row, TILE), :] = weight * face

    def weigh_pack(g):
        for k in range(quad):
            row, at = own_tile(g * quad + k)
            zs_f[0, pl.ds(at, TILE), :] = pack([wbuf[f, pl.ds(row, TILE), :] for f in range(fields)], 0)

    def quota_stages(low, high, with_ends):
        n = high - low
        base = low if low == 0 else low - 1

        def main(x):
            for k in range(tiles):
                row, at = own_tile(x * tiles + k)
                own = pl.ds(at, TILE)
                right, left, middle = shifted[0, own, :], shifted[1, own, :], codes[0, pl.ds(row, TILE), :]
                sums = taps(row, 1, lambda near: left, lambda near: middle, lambda near: right, wbuf, low, high)
                for m in range(3):
                    for f in range(n):
                        parts_f[k, m, f] = sums[m][f]
                if with_ends:
                    value = edge[own, :]
                    ends[own, :] = packed_taps(row, 1, lambda near: value, wbuf, fields)

        def close(x):
            for k in range(tiles):
                row, at = own_tile(x * tiles + k)
                own = pl.ds(at, TILE)
                packed = ends[own, :]
                found = []
                for f in range(n):
                    spread = pltpu.roll(packed, LANES - 1 - 2 * (low + f), 1)
                    total = parts_f[k, 1, f] + pltpu.roll(parts_f[k, 2, f], LANES - 1, 1)
                    total = total + pltpu.roll(parts_f[k, 0, f], 1, 1)
                    found.append(total + jnp.where(both_ends, spread, 0.0))
                if with_ends:
                    inverted = 1.0 / found[flux]
                    weights[own, :] = inverted
                    found = found[:flux]
                else:
                    inverted = weights[own, :]
                for f, value in enumerate(found):
                    qbuf[base + f, pl.ds(row, TILE), :] = value * inverted

        def send_pack(x):
            for k in range(tiles):
                row, at = own_tile(x * tiles + k)
                group = group_a if with_ends else group_b
                zs_f[1 if with_ends else 2, pl.ds(at, TILE), :] = pack([qbuf[s, pl.ds(row, TILE), :] for s in group], 0)

        return [main, close, send_pack]

    def scatter_stages(group, plane):
        n = len(group)
        low = group[0]

        def main(x):
            for k in range(tiles):
                row, at = own_tile(x * tiles + k)
                own_code = {}

                def source(near):
                    return codes[0, near, :]

                sums = taps(row, -1, source, source, source, qbuf, low, low + n)
                for m in range(3):
                    for f in range(n):
                        parts_f[k, m, f] = sums[m][f]
                parts_f[k, 0, n] = packed_taps(row, -1, lambda near: codes[1, near, :], qbuf, plane)

        def close(x):
            for k in range(tiles):
                row, at = own_tile(x * tiles + k)
                own = pl.ds(at, TILE)
                packed = parts_f[k, 0, n]
                factor = scaling[own, :]
                for f, s in enumerate(group):
                    spread = pltpu.roll(packed, LANES - 1 - 2 * f, 1)
                    total = parts_f[k, 1, f]
                    total = total + jnp.where(first_lane, spread, pltpu.roll(parts_f[k, 2, f], 1, 1))
                    total = total + jnp.where(last_lane, spread, pltpu.roll(parts_f[k, 0, f], LANES - 1, 1))
                    out[s, own, :] = factor * total

        return [main, close]

    blank(codes, 0, 2)
    blank(wbuf, 0, fields + 1)
    blank(qbuf, 0, nspec + 2)
    loads[0].wait()
    loads[1].wait()
    lax.fori_loop(0, count, fill, 0, unroll=8)
    pl.semaphore_wait(barrier, len(others))
    code_z.start()
    code_own.start()
    for copy in loads[2:]:
        copy.wait()
    totals = tuple(jnp.zeros((TILE, LANES), jnp.float32) for _ in range(nspec))
    totals = lax.fori_loop(0, count // 8 * 4, add_up, totals, unroll=4)
    code_z.receive()
    code_packed.start()
    totals = lax.fori_loop(count // 8 * 4, count, add_up, totals, unroll=4)
    local = jnp.concatenate(
        [jnp.sum(total, axis=0, keepdims=True) for total in totals]
        + [jnp.zeros((peers.shape[2] - nspec, LANES), jnp.float32)],
        axis=0,
    )
    reduce_start("gx", local)
    code_own.receive()
    code_packed.receive()
    pipelined([count_taps, weigh, weigh_pack], count // quad)
    w_z.start()
    w_a.start()
    w_b.start()
    reduce_start("gy", reduce_finish("gx"))
    w_z.receive()
    w_packed.start()
    w_a.receive()
    w_packed.receive()
    pipelined(quota_stages(0, cut + 1, True), nx)
    qa_z.start()
    q_a.start()
    w_b.receive()
    reduce_start("gz", reduce_finish("gy"))

    def middle_a():
        qa_z.receive()
        qa_packed.start()

    pipelined(quota_stages(cut + 1, fields, False), nx, (nx // 3, middle_a))
    qb_z.start()
    q_b.start()
    summed = reduce_finish("gz")
    change[...] = jnp.broadcast_to(jnp.sum(summed, axis=1, keepdims=True) * scale, change.shape)
    q_a.receive()
    qa_packed.receive()

    def middle_b():
        qb_z.receive()
        qb_packed.start()

    pipelined(scatter_stages(group_a, nspec), nx, (nx // 3, middle_b))
    save_a = pltpu.make_async_copy(out.at[pl.ds(0, cut)], out_h.at[pl.ds(0, cut)], store.at[0])
    save_a.start()
    q_b.receive()
    qb_packed.receive()
    pipelined(scatter_stages(group_b, nspec + 1), nx)
    save_b = pltpu.make_async_copy(out.at[pl.ds(cut, nspec - cut)], out_h.at[pl.ds(cut, nspec - cut)], store.at[1])
    save_b.start()
    for part in everything:
        part.finish()
    save_a.wait()
    save_b.wait()


def per_device(provisional, cut_flag, cut_code, volume_level, area_level):
    nspec, nx, ny, nz = provisional.shape
    assert nz == LANES and ny % TILE == 0 and nx % TILE == 0
    own = nx * ny
    tiles = ny // TILE
    rows = TILE + (nx + 2) * (ny + TILE)
    most = max(lax.axis_size(axis) for axis in AXES)
    cells = own * nz * math.prod(lax.axis_size(axis) for axis in AXES)
    high = -(-nspec // TILE) * TILE
    cut = nspec // 2
    fields = nspec + 1
    group = max(cut + 1, nspec - cut)
    wide = -(-group // TILE) * TILE
    f32, i32 = jnp.float32, jnp.int32
    vmem = pl.BlockSpec(memory_space=pltpu.VMEM)
    hbm = pl.BlockSpec(memory_space=pl.ANY)
    shapes = [
        ((nspec, own, nz), f32), ((own, nz), i32), ((own, nz), i32), ((own, nz), i32), ((own, nz), i32),
        ((nspec, own, nz), f32),
        ((2, rows, nz), i32), ((fields + 1, rows, nz), f32), ((nspec + 2, rows, nz), f32),
        ((2, own, nz), i32), ((own, nz), i32),
        ((own, nz), i32), ((own, nz), i32), ((own, nz), i32),
        ((3, own, nz), f32), ((3, own, nz), f32), ((3, own, nz), f32),
        ((2, 2, nx, nz), i32), ((2, 2, nx, nz), i32), ((2, 4, TILE, nz), i32), ((2, 4, TILE, nz), i32),
        ((2, fields + 1, nx, nz), f32), ((2, fields + 1, nx, nz), f32), ((3, 4, wide, nz), f32), ((3, 4, wide, nz), f32),
        ((2, nspec + 2, nx, nz), f32), ((2, nspec + 2, nx, nz), f32), ((4, 4, wide, nz), f32), ((4, 4, wide, nz), f32),
        ((own, nz), f32), ((own, nz), f32), ((own, nz), f32),
        ((4, 4, TILE, nz), i32), ((tiles, 3, group + 1, TILE, nz), f32),
        ((3, most, high, nz), f32),
    ]
    dma = pltpu.SemaphoreType.DMA
    out, change = pl.pallas_call(
        functools.partial(kernel, nx, ny, 1.0 / math.sqrt(cells)),
        out_shape=(
            jax.ShapeDtypeStruct((nspec, own, nz), f32),
            jax.ShapeDtypeStruct((high, nz), f32),
        ),
        in_specs=[hbm] * 5,
        out_specs=(hbm, vmem),
        scratch_shapes=[pltpu.VMEM(shape, kind) for shape, kind in shapes]
        + [
            dma((5,)), dma((2,)), dma((4, 2)), dma((4, 2)), dma((9, 8)), dma((9, 8)), dma((3, most)), dma((3, most)),
        ],
        compiler_params=pltpu.CompilerParams(
            collective_id=0, has_side_effects=True, vmem_limit_bytes=60 * 1024 * 1024
        ),
    )(
        provisional.reshape(nspec, own, nz),
        cut_flag.reshape(own, nz),
        cut_code.reshape(own, nz),
        volume_level.reshape(own, nz),
        area_level.reshape(own, nz),
    )
    return out.reshape(provisional.shape), change[:nspec, 0]


def solution(mesh):
    spec = P("gx", "gy", "gz")
    wide = P(None, "gx", "gy", "gz")
    return jax.shard_map(
        per_device, mesh=mesh, in_specs=(wide, spec, spec, spec, spec), out_specs=(wide, P()), check_vma=False
    )
```

time: 70.8 us -> 50.9 us (0.72)
  Pallas kernels: 65.4 us -> 45.6 us
    pallas_call x1, Pallas kernels: 65.4 us -> 45.6 us  [per_device(): pl.pallas_call(functools.partial(kernel, nx, ny, 1.0 / math.sqrt(cells)),...]
where the time goes in v1:
time: 50.9 us; the launch traced here: 50.8 us
  Pallas kernels  45.6 us (90%)
  local copies, waits for them, and re-layouts  4.54 us (9%)
  between operations  0.64 us (1%)
    pallas_call x1, Pallas kernels, per_device(): pl.pallas_call(functools.partial(kernel, nx, ny, 1.0 / math.sqrt(cells)),...  45.6 us
    unnamed x1, local copies, waits for them, and re-layouts  3.22 us
    slice x1, local copies, waits for them, and re-layouts, per_device(): return (out.reshape(provisional.shape), change[:nspec, 0])  1.32 us

profile of v1, /device:TPU:0, one launch (start us, length us, event | category | flops | bytes accessed | tf_op | source)
XLA Modules:
  0.0 50.8 jit_solution(16868579410566225361)
XLA Ops:
  0.6 45.6 %shard_map.68 = (f32[9,512,128]{2,1,0:T(8,128)}, f32[16,128]{1,0:T(8,128)}) custom-call(f32[9,512,128]{2,1,0:T(8,128)} %bitcast.7, s32[512,128]{1,0:T(8,128)} %bitcast.8, s32[512,128]{1,0:T(8,128)} %bitcast.9, s32[512,128]{1,0:T(8,128)} %bitcast.10, s32[512,128]{1,0:T(8,128)} %bitcast.11), custom_call_target="tpu_custom_call" | custom-call | tf_op jit(solution)/shard_map/pallas_call | solution.py:578
  46.2 1.3 %slice_reduce_fusion = f32[9]{0:T(128)} fusion(f32[16,128]{1,0:T(8,128)} %get-tuple-element.5), kind=kLoop, calls=%fused_computation | loop fusion | bytes 72 | tf_op jit(solution)/shard_map/slice | solution.py:600
  47.5 3.2 %copy.8 = f32[9,32,16,128]{3,2,1,0:T(8,128)} copy(f32[9,32,16,128]{3,2,1,0:T(8,128)} %bitcast.6) | data formatting | bytes 4718592

commit v2 on v1

--- a/solution.py
+++ b/solution.py
@@ -28,13 +28,16 @@
         step(i, 0, i + 1)
 
     def body(i, carry):
-        if hook is not None:
-            at, action = hook
-            pl.when(i == at)(action)
         step(i, 0, depth)
         return carry
 
-    lax.fori_loop(depth - 1, count, body, 0)
+    low = depth - 1
+    if hook is not None:
+        at, action = hook
+        lax.fori_loop(low, at, body, 0)
+        action()
+        low = at
+    lax.fori_loop(low, count, body, 0)
     for i in range(count, count + depth - 1):
         step(i, i - count + 1, depth)
 
@@ -42,18 +45,17 @@
 def kernel(
     nx, ny, scale,
     prov_h, flag_h, code_h, vol_h, area_h,
-    out_h, change,
-    prov, flag, code, vol, area, out,
+    out, change,
+    prov, flag, code, vol, area,
     codes, wbuf, qbuf, shifted, edge,
     zs_i, zl_i, zr_i, zs_f, zl_f, zr_f,
     ys_i, yr_i, cs_i, cr_i, ys_w, yr_w, cs_w, cr_w, ys_q, yr_q, cs_q, cr_q,
     weights, scaling, ends, parts_i, parts_f, peers,
-    load, store, z_send, z_recv, send, recv, peer_send, peer_recv,
+    load, z_send, z_recv, send, recv, peer_send, peer_recv,
 ):
     nspec = prov.shape[0]
     pitch = ny + TILE
     tiles = ny // TILE
-    count = nx * tiles
     here = {axis: lax.axis_index(axis) for axis in AXES}
     size = {axis: lax.axis_size(axis) for axis in AXES}
     lane = lax.broadcasted_iota(jnp.int32, (TILE, LANES), 1)
@@ -92,9 +94,12 @@
     def first(x):
         return TILE + x * pitch
 
-    def own_tile(t):
-        row = TILE + (t // tiles + 1) * pitch + lax.rem(t, tiles) * TILE
-        return pl.multiple_of(row, TILE), pl.multiple_of(t * TILE, TILE)
+    def own_tile(x, k):
+        row = (TILE + pitch + k * TILE) + x * pitch
+        at = x * ny + k * TILE
+        if isinstance(x, int):
+            return row, at
+        return pl.multiple_of(row, TILE), pl.multiple_of(at, TILE)
 
     def side(axis, step):
         return here[axis] < size[axis] - 1 if step > 0 else here[axis] > 0
@@ -238,14 +243,15 @@
             pl.when(above_z)(self.copies[1].wait_recv)
             zero = jnp.zeros((TILE, LANES), self.buf.dtype)
 
-            def place(t, carry):
-                row, at = own_tile(t)
-                low = jnp.where(below_z, self.zl[pl.ds(at, TILE), :], zero)
-                high = jnp.where(above_z, self.zr[pl.ds(at, TILE), :], zero)
-                self.buf[self.plane, pl.ds(row, TILE), :] = jnp.where(odd, low, high)
+            def place(x, carry):
+                for k in range(tiles):
+                    row, at = own_tile(x, k)
+                    low = jnp.where(below_z, self.zl[pl.ds(at, TILE), :], zero)
+                    high = jnp.where(above_z, self.zr[pl.ds(at, TILE), :], zero)
+                    self.buf[self.plane, pl.ds(row, TILE), :] = jnp.where(odd, low, high)
                 return carry
 
-            lax.fori_loop(0, count, place, 0, unroll=8)
+            lax.fori_loop(0, nx, place, 0, unroll=8)
 
         def finish(self):
             pl.when(above_z)(self.copies[0].wait_send)
@@ -297,24 +303,27 @@
         face = jnp.where(is_cut, area[own, :], 256).astype(jnp.float32) * (1.0 / 256.0)
         return volume, face
 
-    def fill(t, carry):
-        row, at = own_tile(t)
-        own = pl.ds(at, TILE)
-        value = jnp.where(flag[own, :] == 1, code[own, :] | CENTER, CENTER)
-        codes[0, pl.ds(row, TILE), :] = value
-        shifted[0, own, :] = jnp.where(first_lane, 0, pltpu.roll(value, 1, 1))
-        shifted[1, own, :] = jnp.where(last_lane, 0, pltpu.roll(value, LANES - 1, 1))
-        low = jnp.broadcast_to(value[:, :1], (TILE, LANES))
-        high = lax.shift_right_logical(jnp.broadcast_to(value[:, LANES - 1:], (TILE, LANES)), 2)
-        zs_i[own, :] = jnp.where(odd, high, low)
-        edge[own, :] = jnp.where(odd, low, high)
+    def fill(x, carry):
+        for k in range(tiles):
+            row, at = own_tile(x, k)
+            own = pl.ds(at, TILE)
+            value = jnp.where(flag[own, :] == 1, code[own, :] | CENTER, CENTER)
+            codes[0, pl.ds(row, TILE), :] = value
+            shifted[0, own, :] = jnp.where(first_lane, 0, pltpu.roll(value, 1, 1))
+            shifted[1, own, :] = jnp.where(last_lane, 0, pltpu.roll(value, LANES - 1, 1))
+            low = jnp.broadcast_to(value[:, :1], (TILE, LANES))
+            high = lax.shift_right_logical(jnp.broadcast_to(value[:, LANES - 1:], (TILE, LANES)), 2)
+            zs_i[own, :] = jnp.where(odd, high, low)
+            edge[own, :] = jnp.where(odd, low, high)
         return carry
 
-    def add_up(t, totals):
-        _, at = own_tile(t)
-        own = pl.ds(at, TILE)
-        volume, _ = fractions(own)
-        return tuple(totals[s] + volume * prov[s, own, :] for s in range(nspec))
+    def add_up(x, totals):
+        for k in range(tiles):
+            _, at = own_tile(x, k)
+            own = pl.ds(at, TILE)
+            volume, _ = fractions(own)
+            totals = tuple(totals[s] + volume * prov[s, own, :] for s in range(nspec))
+        return totals
 
     def taps(row, step, left, middle, right, buf, low, high):
         zero = jnp.zeros((TILE, LANES), jnp.float32)
@@ -353,11 +362,12 @@
             packed = jnp.where(lane == 2 * f + 1, pltpu.roll(value, 2 * f + 2, 1), packed)
         return packed
 
-    quad = 4
+    quad = 2
+    members = [(k, k // tiles, k % tiles) for k in range(quad * tiles)]
 
     def count_taps(g):
-        for k in range(quad):
-            row, at = own_tile(g * quad + k)
+        for k, x, y in members:
+            row, at = own_tile(g * quad + x, y)
             sums = [None] * 3
             total = None
             for a, b, position in BLOCK:
@@ -375,8 +385,8 @@
             parts_i[k, 3] = total
 
     def weigh(g):
-        for k in range(quad):
-            row, at = own_tile(g * quad + k)
+        for k, x, y in members:
+            row, at = own_tile(g * quad + x, y)
             own = pl.ds(at, TILE)
             from_end = pltpu.roll(parts_i[k, 3], LANES - 1, 1)
             from_left = pltpu.roll(lax.shift_right_logical(parts_i[k, 2], 2), 1, 1)
@@ -393,8 +403,8 @@
             wbuf[flux, pl.ds(row, TILE), :] = weight * face
 
     def weigh_pack(g):
-        for k in range(quad):
-            row, at = own_tile(g * quad + k)
+        for k, x, y in members:
+            row, at = own_tile(g * quad + x, y)
             zs_f[0, pl.ds(at, TILE), :] = pack([wbuf[f, pl.ds(row, TILE), :] for f in range(fields)], 0)
 
     def quota_stages(low, high, with_ends):
@@ -403,7 +413,7 @@
 
         def main(x):
             for k in range(tiles):
-                row, at = own_tile(x * tiles + k)
+                row, at = own_tile(x, k)
                 own = pl.ds(at, TILE)
                 right, left, middle = shifted[0, own, :], shifted[1, own, :], codes[0, pl.ds(row, TILE), :]
                 sums = taps(row, 1, lambda near: left, lambda near: middle, lambda near: right, wbuf, low, high)
@@ -416,7 +426,7 @@
 
         def close(x):
             for k in range(tiles):
-                row, at = own_tile(x * tiles + k)
+                row, at = own_tile(x, k)
                 own = pl.ds(at, TILE)
                 packed = ends[own, :]
                 found = []
@@ -436,7 +446,7 @@
 
         def send_pack(x):
             for k in range(tiles):
-                row, at = own_tile(x * tiles + k)
+                row, at = own_tile(x, k)
                 group = group_a if with_ends else group_b
                 zs_f[1 if with_ends else 2, pl.ds(at, TILE), :] = pack([qbuf[s, pl.ds(row, TILE), :] for s in group], 0)
 
@@ -448,8 +458,7 @@
 
         def main(x):
             for k in range(tiles):
-                row, at = own_tile(x * tiles + k)
-                own_code = {}
+                row, at = own_tile(x, k)
 
                 def source(near):
                     return codes[0, near, :]
@@ -462,7 +471,7 @@
 
         def close(x):
             for k in range(tiles):
-                row, at = own_tile(x * tiles + k)
+                row, at = own_tile(x, k)
                 own = pl.ds(at, TILE)
                 packed = parts_f[k, 0, n]
                 factor = scaling[own, :]
@@ -480,17 +489,17 @@
     blank(qbuf, 0, nspec + 2)
     loads[0].wait()
     loads[1].wait()
-    lax.fori_loop(0, count, fill, 0, unroll=8)
+    lax.fori_loop(0, nx, fill, 0, unroll=8)
     pl.semaphore_wait(barrier, len(others))
     code_z.start()
     code_own.start()
     for copy in loads[2:]:
         copy.wait()
     totals = tuple(jnp.zeros((TILE, LANES), jnp.float32) for _ in range(nspec))
-    totals = lax.fori_loop(0, count // 8 * 4, add_up, totals, unroll=4)
+    totals = lax.fori_loop(0, nx // 2, add_up, totals, unroll=2)
     code_z.receive()
     code_packed.start()
-    totals = lax.fori_loop(count // 8 * 4, count, add_up, totals, unroll=4)
+    totals = lax.fori_loop(nx // 2, nx, add_up, totals, unroll=2)
     local = jnp.concatenate(
         [jnp.sum(total, axis=0, keepdims=True) for total in totals]
         + [jnp.zeros((peers.shape[2] - nspec, LANES), jnp.float32)],
@@ -499,7 +508,7 @@
     reduce_start("gx", local)
     code_own.receive()
     code_packed.receive()
-    pipelined([count_taps, weigh, weigh_pack], count // quad)
+    pipelined([count_taps, weigh, weigh_pack], nx // quad)
     w_z.start()
     w_a.start()
     w_b.start()
@@ -531,17 +540,11 @@
         qb_packed.start()
 
     pipelined(scatter_stages(group_a, nspec), nx, (nx // 3, middle_b))
-    save_a = pltpu.make_async_copy(out.at[pl.ds(0, cut)], out_h.at[pl.ds(0, cut)], store.at[0])
-    save_a.start()
     q_b.receive()
     qb_packed.receive()
     pipelined(scatter_stages(group_b, nspec + 1), nx)
-    save_b = pltpu.make_async_copy(out.at[pl.ds(cut, nspec - cut)], out_h.at[pl.ds(cut, nspec - cut)], store.at[1])
-    save_b.start()
     for part in everything:
         part.finish()
-    save_a.wait()
-    save_b.wait()
 
 
 def per_device(provisional, cut_flag, cut_code, volume_level, area_level):
@@ -559,10 +562,9 @@
     wide = -(-group // TILE) * TILE
     f32, i32 = jnp.float32, jnp.int32
     vmem = pl.BlockSpec(memory_space=pltpu.VMEM)
-    hbm = pl.BlockSpec(memory_space=pl.ANY)
+    hbm = pl.BlockSpec(memory_space=pltpu.HBM)
     shapes = [
         ((nspec, own, nz), f32), ((own, nz), i32), ((own, nz), i32), ((own, nz), i32), ((own, nz), i32),
-        ((nspec, own, nz), f32),
         ((2, rows, nz), i32), ((fields + 1, rows, nz), f32), ((nspec + 2, rows, nz), f32),
         ((2, own, nz), i32), ((own, nz), i32),
         ((own, nz), i32), ((own, nz), i32), ((own, nz), i32),
@@ -571,7 +573,7 @@
         ((2, fields + 1, nx, nz), f32), ((2, fields + 1, nx, nz), f32), ((3, 4, wide, nz), f32), ((3, 4, wide, nz), f32),
         ((2, nspec + 2, nx, nz), f32), ((2, nspec + 2, nx, nz), f32), ((4, 4, wide, nz), f32), ((4, 4, wide, nz), f32),
         ((own, nz), f32), ((own, nz), f32), ((own, nz), f32),
-        ((4, 4, TILE, nz), i32), ((tiles, 3, group + 1, TILE, nz), f32),
+        ((2 * tiles, 4, TILE, nz), i32), ((tiles, 3, group + 1, TILE, nz), f32),
         ((3, most, high, nz), f32),
     ]
     dma = pltpu.SemaphoreType.DMA
@@ -582,20 +584,21 @@
             jax.ShapeDtypeStruct((high, nz), f32),
         ),
         in_specs=[hbm] * 5,
-        out_specs=(hbm, vmem),
+        out_specs=(vmem, vmem),
         scratch_shapes=[pltpu.VMEM(shape, kind) for shape, kind in shapes]
         + [
-            dma((5,)), dma((2,)), dma((4, 2)), dma((4, 2)), dma((9, 8)), dma((9, 8)), dma((3, most)), dma((3, most)),
+            dma((5,)), dma((4, 2)), dma((4, 2)), dma((9, 8)), dma((9, 8)), dma((3, most)), dma((3, most)),
         ],
         compiler_params=pltpu.CompilerParams(
-            collective_id=0, has_side_effects=True, vmem_limit_bytes=60 * 1024 * 1024
+            collective_id=0, has_side_effects=True, vmem_limit_bytes=26 * 1024 * 1024
         ),
     )(
+        *[pltpu.with_memory_space_constraint(x, pltpu.HBM) for x in (
         provisional.reshape(nspec, own, nz),
         cut_flag.reshape(own, nz),
         cut_code.reshape(own, nz),
         volume_level.reshape(own, nz),
-        area_level.reshape(own, nz),
+        area_level.reshape(own, nz))]
     )
     return out.reshape(provisional.shape), change[:nspec, 0]
 

time: 50.9 us -> 44.6 us (0.88)
  Pallas kernels: 45.6 us -> 41.8 us
  local copies, waits for them, and re-layouts: 4.54 us -> 2.03 us
    pallas_call x1, Pallas kernels: 45.6 us -> 41.8 us  [per_device(): pl.pallas_call(functools.partial(kernel, nx, ny, 1.0 / math.sqrt(cells)),...]
    unnamed x1, local copies, waits for them, and re-layouts: 3.22 us -> 1.4 us
    slice x1, local copies, waits for them, and re-layouts: 1.32 us -> 0.63 us  [per_device(): return (out.reshape(provisional.shape), change[:nspec, 0])]
where the time goes in v2:
time: 44.6 us; the launch traced here: 44.5 us
  Pallas kernels  41.8 us (94%)
  local copies, waits for them, and re-layouts  2.03 us (5%)
  between operations  0.64 us (1%)
    pallas_call x1, Pallas kernels, per_device(): pl.pallas_call(functools.partial(kernel, nx, ny, 1.0 / math.sqrt(cells)),...  41.8 us
    unnamed x1, local copies, waits for them, and re-layouts  1.4 us

profile of v2, /device:TPU:0, one launch (start us, length us, event | category | flops | bytes accessed | tf_op | source)
XLA Modules:
  0.0 44.5 jit_solution(14722322775257084503)
XLA Ops:
  0.6 41.8 %shard_map.68 = (f32[9,512,128]{2,1,0:T(8,128)S(1)}, f32[16,128]{1,0:T(8,128)S(1)}) custom-call(f32[9,512,128]{2,1,0:T(8,128)} %bitcast.7, s32[512,128]{1,0:T(8,128)} %bitcast.8, s32[512,128]{1,0:T(8,128)} %bitcast.9, s32[512,128]{1,0:T(8,128)} %bitcast.10, s32[512,128]{1,0:T(8,128)} %bitcast.11), custom_call_target="tpu_custom_call" | custom-call | tf_op jit(solution)/shard_map/pallas_call | solution.py:580
  42.5 0.6 %slice_reduce_fusion = f32[9]{0:T(128)} fusion(f32[16,128]{1,0:T(8,128)S(1)} %get-tuple-element.5), kind=kLoop, calls=%fused_computation | loop fusion | bytes 72 | tf_op jit(solution)/shard_map/slice | solution.py:603
  43.1 1.4 %copy.8 = f32[9,32,16,128]{3,2,1,0:T(8,128)} copy(f32[9,32,16,128]{3,2,1,0:T(8,128)S(1)} %bitcast.6) | data formatting | bytes 4718592

commit v3 on v2

--- a/solution.py
+++ b/solution.py
@@ -47,10 +47,11 @@
     prov_h, flag_h, code_h, vol_h, area_h,
     out, change,
     prov, flag, code, vol, area,
-    codes, wbuf, qbuf, shifted, edge,
+    codes, wbuf, qbuf, packed, shifted, edge,
     zs_i, zl_i, zr_i, zs_f, zl_f, zr_f,
-    ys_i, yr_i, cs_i, cr_i, ys_w, yr_w, cs_w, cr_w, ys_q, yr_q, cs_q, cr_q,
-    weights, scaling, ends, parts_i, parts_f, peers,
+    ys_i, yr_i, cs_i, cr_i, ys_p, yr_p, cs_p, cr_p,
+    xr, ys, yr, cs, cr,
+    gathered, scaling, parts_i, parts_f, parts_e, peers,
     load, z_send, z_recv, send, recv, peer_send, peer_recv,
 ):
     nspec = prov.shape[0]
@@ -63,10 +64,8 @@
     first_lane = lane == 0
     last_lane = lane == LANES - 1
     both_ends = first_lane | last_lane
-    cut = nspec // 2
-    flux = cut
     fields = nspec + 1
-    group_a, group_b = list(range(cut)), list(range(cut, nspec))
+    flux = nspec
 
     inputs = [(flag_h, flag), (code_h, code), (vol_h, vol), (area_h, area), (prov_h, prov)]
     loads = [pltpu.make_async_copy(src, dst, load.at[k]) for k, (src, dst) in enumerate(inputs)]
@@ -257,20 +256,104 @@
             pl.when(above_z)(self.copies[0].wait_send)
             pl.when(below_z)(self.copies[1].wait_send)
 
+    class Faces:
+        def __init__(self, number, buf, n, which):
+            self.buf, self.n = buf, n
+            self.xr, self.ys, self.yr, self.cs, self.cr = xr.at[which], ys.at[which], yr.at[which], cs.at[which], cr.at[which]
+            self.copies = []
+            for k, (dx, dy) in enumerate(WAYS):
+                way = 0 if dx + dy > 0 else 1
+                if dy == 0:
+                    source = buf.at[pl.ds(0, n), pl.ds(first(nx if dx > 0 else 1), ny), :]
+                    landing = self.xr.at[way, pl.ds(0, n), pl.ds(TILE, ny), :]
+                elif dx == 0:
+                    source = self.ys.at[way, pl.ds(0, n)]
+                    landing = self.yr.at[way, pl.ds(0, n), pl.ds(TILE, nx), :]
+                else:
+                    source, landing = self.cs.at[k - 4], self.cr.at[k - 4]
+                self.copies.append(
+                    pltpu.make_async_remote_copy(
+                        src_ref=source, dst_ref=landing,
+                        send_sem=send.at[number, k], recv_sem=recv.at[number, k],
+                        device_id={"gx": moved("gx", dx), "gy": moved("gy", dy)}, device_id_type=MESH,
+                    )
+                )
+
+        def blank(self):
+            def low(f, carry):
+                zeros = jnp.zeros((TILE, LANES), jnp.float32)
+                for p in range(nx + 3):
+                    self.buf[f, pl.ds(p * pitch, TILE), :] = zeros
+                for p in (0, nx + 1):
+                    for k in range(tiles):
+                        self.buf[f, pl.ds(first(p) + k * TILE, TILE), :] = zeros
+                for way in range(2):
+                    for at in (0, TILE + ny):
+                        self.xr[way, f, pl.ds(at, TILE), :] = zeros
+                    for at in (0, TILE + nx):
+                        self.yr[way, f, pl.ds(at, TILE), :] = zeros
+                return carry
+
+            lax.fori_loop(0, self.n, low, 0)
+
+            def clear(ref, way, extent):
+                def body(f, carry):
+                    ref[way, f, pl.ds(TILE, extent), :] = jnp.zeros((extent, LANES), jnp.float32)
+                    return carry
+                lax.fori_loop(0, self.n, body, 0)
+
+            for way, step in ((0, 1), (1, -1)):
+                pl.when(jnp.logical_not(exists(-step, 0)))(functools.partial(clear, self.xr, way, ny))
+                pl.when(jnp.logical_not(exists(0, -step)))(functools.partial(clear, self.yr, way, nx))
+
+        def start(self):
+            buf = self.buf
+
+            def gather(f, carry):
+                for x in range(0, nx, TILE):
+                    for way, step in ((0, 1), (1, -1)):
+                        self.ys[way, f, pl.ds(x, TILE), :] = buf[f, pl.ds(first(x + 1) + edge_row(step), TILE, stride=pitch), :]
+                for k, (dx, dy) in enumerate(WAYS[4:]):
+                    row = first(nx if dx > 0 else 1) + edge_row(dy)
+                    self.cs[k, pl.ds(f, 1), :] = buf[f, pl.ds(row, 1), :]
+                return carry
+
+            for k in range(2):
+                pl.when(exists(*WAYS[k]))(self.copies[k].start)
+            lax.fori_loop(0, self.n, gather, 0)
+            for k in range(2, 8):
+                pl.when(exists(*WAYS[k]))(self.copies[k].start)
+
+        def receive(self):
+            for k, (dx, dy) in enumerate(WAYS):
+                pl.when(exists(-dx, -dy))(self.copies[k].wait_recv)
+
+            def corner(k, dx, dy):
+                way = 0 if dy > 0 else 1
+                at = TILE - 1 if dx > 0 else TILE + nx
+
+                def body(f, carry):
+                    self.yr[way, f, pl.ds(at, 1), :] = self.cr[k, pl.ds(f, 1), :]
+                    return carry
+                lax.fori_loop(0, self.n, body, 0)
+
+            for k, (dx, dy) in enumerate(WAYS[4:]):
+                pl.when(exists(-dx, -dy))(functools.partial(corner, k, dx, dy))
+
+        def finish(self):
+            for k, (dx, dy) in enumerate(WAYS):
+                pl.when(exists(dx, dy))(self.copies[k].wait_send)
+
     code_z = Depth(0, zs_i, zl_i, zr_i, codes, 1)
     code_own = Unit(0, codes, 0, 1, ys_i, yr_i, cs_i, cr_i, 0)
     code_packed = Unit(1, codes, 1, 2, ys_i, yr_i, cs_i, cr_i, 1)
-    w_z = Depth(1, zs_f.at[0], zl_f.at[0], zr_f.at[0], wbuf, fields)
-    w_a = Unit(2, wbuf, 0, cut + 1, ys_w, yr_w, cs_w, cr_w, 0)
-    w_b = Unit(3, wbuf, cut + 1, fields, ys_w, yr_w, cs_w, cr_w, 1)
-    w_packed = Unit(4, wbuf, fields, fields + 1, ys_w, yr_w, cs_w, cr_w, 2)
-    qa_z = Depth(2, zs_f.at[1], zl_f.at[1], zr_f.at[1], qbuf, nspec)
-    q_a = Unit(5, qbuf, 0, cut, ys_q, yr_q, cs_q, cr_q, 0)
-    qa_packed = Unit(6, qbuf, nspec, nspec + 1, ys_q, yr_q, cs_q, cr_q, 1)
-    qb_z = Depth(3, zs_f.at[2], zl_f.at[2], zr_f.at[2], qbuf, nspec + 1)
-    q_b = Unit(7, qbuf, cut, nspec, ys_q, yr_q, cs_q, cr_q, 2)
-    qb_packed = Unit(8, qbuf, nspec + 1, nspec + 2, ys_q, yr_q, cs_q, cr_q, 3)
-    everything = [code_z, code_own, code_packed, w_z, w_a, w_b, w_packed, qa_z, q_a, qa_packed, qb_z, q_b, qb_packed]
+    w_z = Depth(1, zs_f.at[0], zl_f.at[0], zr_f.at[0], packed, 0)
+    w_all = Faces(2, wbuf, fields, 0)
+    w_packed = Unit(3, packed, 0, 1, ys_p, yr_p, cs_p, cr_p, 0)
+    q_z = Depth(2, zs_f.at[1], zl_f.at[1], zr_f.at[1], packed, 1)
+    q_all = Faces(4, qbuf, nspec, 1)
+    q_packed = Unit(5, packed, 1, 2, ys_p, yr_p, cs_p, cr_p, 1)
+    everything = [code_z, code_own, code_packed, w_z, w_all, w_packed, q_z, q_all, q_packed]
 
     def peer_copies(axis):
         number = AXES.index(axis)
@@ -325,24 +408,33 @@
             totals = tuple(totals[s] + volume * prov[s, own, :] for s in range(nspec))
         return totals
 
-    def taps(row, step, left, middle, right, buf, low, high):
+    def masked_sums(taps, low, high):
         zero = jnp.zeros((TILE, LANES), jnp.float32)
         sums = [[None] * (high - low) for _ in range(3)]
-        for a, b, position in BLOCK:
-            near = pl.ds(row + step * (a * pitch + b), TILE)
-            present = []
-            for k, source in enumerate((left, middle, right)):
-                if step > 0 and position + k == 13:
-                    present.append(None)
-                else:
-                    present.append((source(near) & (1 << (position + k))) != 0)
+        for sources, position, value_of in taps:
+            present = [
+                None if source is None else (source & (1 << (position + k))) != 0 for k, source in enumerate(sources)
+            ]
             for f in range(low, high):
-                value = buf[f, near, :]
+                value = value_of(f)
                 for k in range(3):
                     term = value if present[k] is None else jnp.where(present[k], value, zero)
                     old = sums[k][f - low]
                     sums[k][f - low] = term if old is None else old + term
         return sums
+
+    def keep_sums(slot, sums, low):
+        for m in range(3):
+            for f, value in enumerate(sums[m]):
+                parts_f[slot, m, low + f] = value
+
+    def merged(slot, f, wrap):
+        if wrap:
+            up, down = pltpu.roll(parts_f[slot, 2, f], 1, 1), pltpu.roll(parts_f[slot, 0, f], LANES - 1, 1)
+            up, down = jnp.where(first_lane, 0.0, up), jnp.where(last_lane, 0.0, down)
+        else:
+            up, down = pltpu.roll(parts_f[slot, 2, f], LANES - 1, 1), pltpu.roll(parts_f[slot, 0, f], 1, 1)
+        return parts_f[slot, 1, f] + up + down
 
     def packed_taps(row, step, source, buf, plane):
         zero = jnp.zeros((TILE, LANES), jnp.float32)
@@ -398,8 +490,7 @@
             scaling[own, :] = face * share
             weight = volume * share
             for s in range(nspec):
-                f = s if s < cut else s + 1
-                wbuf[f, pl.ds(row, TILE), :] = weight * prov[s, own, :]
+                wbuf[s, pl.ds(row, TILE), :] = weight * prov[s, own, :]
             wbuf[flux, pl.ds(row, TILE), :] = weight * face
 
     def weigh_pack(g):
@@ -407,86 +498,159 @@
             row, at = own_tile(g * quad + x, y)
             zs_f[0, pl.ds(at, TILE), :] = pack([wbuf[f, pl.ds(row, TILE), :] for f in range(fields)], 0)
 
-    def quota_stages(low, high, with_ends):
-        n = high - low
-        base = low if low == 0 else low - 1
-
-        def main(x):
-            for k in range(tiles):
-                row, at = own_tile(x, k)
-                own = pl.ds(at, TILE)
-                right, left, middle = shifted[0, own, :], shifted[1, own, :], codes[0, pl.ds(row, TILE), :]
-                sums = taps(row, 1, lambda near: left, lambda near: middle, lambda near: right, wbuf, low, high)
-                for m in range(3):
-                    for f in range(n):
-                        parts_f[k, m, f] = sums[m][f]
-                if with_ends:
-                    value = edge[own, :]
-                    ends[own, :] = packed_taps(row, 1, lambda near: value, wbuf, fields)
-
-        def close(x):
-            for k in range(tiles):
-                row, at = own_tile(x, k)
-                own = pl.ds(at, TILE)
-                packed = ends[own, :]
-                found = []
-                for f in range(n):
-                    spread = pltpu.roll(packed, LANES - 1 - 2 * (low + f), 1)
-                    total = parts_f[k, 1, f] + pltpu.roll(parts_f[k, 2, f], LANES - 1, 1)
-                    total = total + pltpu.roll(parts_f[k, 0, f], 1, 1)
-                    found.append(total + jnp.where(both_ends, spread, 0.0))
-                if with_ends:
-                    inverted = 1.0 / found[flux]
-                    weights[own, :] = inverted
-                    found = found[:flux]
-                else:
-                    inverted = weights[own, :]
-                for f, value in enumerate(found):
-                    qbuf[base + f, pl.ds(row, TILE), :] = value * inverted
-
-        def send_pack(x):
-            for k in range(tiles):
-                row, at = own_tile(x, k)
-                group = group_a if with_ends else group_b
-                zs_f[1 if with_ends else 2, pl.ds(at, TILE), :] = pack([qbuf[s, pl.ds(row, TILE), :] for s in group], 0)
-
-        return [main, close, send_pack]
-
-    def scatter_stages(group, plane):
-        n = len(group)
-        low = group[0]
-
-        def main(x):
-            for k in range(tiles):
-                row, at = own_tile(x, k)
-
-                def source(near):
-                    return codes[0, near, :]
-
-                sums = taps(row, -1, source, source, source, qbuf, low, low + n)
-                for m in range(3):
-                    for f in range(n):
-                        parts_f[k, m, f] = sums[m][f]
-                parts_f[k, 0, n] = packed_taps(row, -1, lambda near: codes[1, near, :], qbuf, plane)
-
-        def close(x):
-            for k in range(tiles):
-                row, at = own_tile(x, k)
-                own = pl.ds(at, TILE)
-                packed = parts_f[k, 0, n]
-                factor = scaling[own, :]
-                for f, s in enumerate(group):
-                    spread = pltpu.roll(packed, LANES - 1 - 2 * f, 1)
-                    total = parts_f[k, 1, f]
-                    total = total + jnp.where(first_lane, spread, pltpu.roll(parts_f[k, 2, f], 1, 1))
-                    total = total + jnp.where(last_lane, spread, pltpu.roll(parts_f[k, 0, f], LANES - 1, 1))
-                    out[s, own, :] = factor * total
-
-        return [main, close]
+    def own_row(t):
+        x, k = lax.div(t, tiles), lax.rem(t, tiles)
+        row = (TILE + pitch) + x * pitch + k * TILE
+        if isinstance(t, int):
+            return int(row), t * TILE
+        return pl.multiple_of(row, TILE), pl.multiple_of(t * TILE, TILE)
+
+    def reader(buf, near):
+        return lambda f: buf[f, near, :]
+
+    def gather_main(t):
+        row, at = own_tile(t // tiles, t % tiles) if isinstance(t, int) else own_row(t)
+        own = pl.ds(at, TILE)
+        right, left, middle = shifted[0, own, :], shifted[1, own, :], codes[0, pl.ds(row, TILE), :]
+        taps = []
+        for a, b, position in BLOCK:
+            center = None if position == 12 else middle
+            taps.append(((left, center, right), position, reader(wbuf, pl.ds(row + a * pitch + b, TILE))))
+        keep_sums(0, masked_sums(taps, 0, fields), 0)
+
+    def gather_close(t):
+        row, at = own_tile(t // tiles, t % tiles) if isinstance(t, int) else own_row(t)
+        for f in range(nspec):
+            qbuf[f, pl.ds(row, TILE), :] = merged(0, f, False)
+        gathered[pl.ds(at, TILE), :] = merged(0, flux, False)
+
+    def gather_strip(j):
+        x = j * TILE
+        for way, (b, y) in enumerate(((-1, 0), (1, ny - 1))):
+            where = pl.ds(x * ny + y, TILE, stride=ny)
+            right, left = shifted[0, where, :], shifted[1, where, :]
+            middle = codes[0, pl.ds(first(1) + x * pitch + y, TILE, stride=pitch), :]
+            taps = []
+            for a in (-1, 0, 1):
+                taps.append(((left, middle, right), 9 * (a + 1) + 3 * (b + 1), reader(yr.at[0, way], pl.ds(TILE + x + a, TILE))))
+            keep_sums(way, masked_sums(taps, 0, fields), 0)
+
+    def gather_strip_close(j):
+        x = j * TILE
+        for way, y in enumerate((0, ny - 1)):
+            rows = pl.ds(first(1) + x * pitch + y, TILE, stride=pitch)
+            for f in range(nspec):
+                qbuf[f, rows, :] = qbuf[f, rows, :] + merged(way, f, False)
+            where = pl.ds(x * ny + y, TILE, stride=ny)
+            gathered[where, :] = gathered[where, :] + merged(way, flux, False)
+
+    def gather_plane(way):
+        a, x = ((-1, 0), (1, nx - 1))[way]
+        for k in range(tiles):
+            row, at = own_tile(x, k)
+            own = pl.ds(at, TILE)
+            right, left, middle = shifted[0, own, :], shifted[1, own, :], codes[0, pl.ds(row, TILE), :]
+            taps = []
+            for b in (-1, 0, 1):
+                taps.append(((left, middle, right), 9 * (a + 1) + 3 * (b + 1), reader(xr.at[0, way], pl.ds(TILE + k * TILE + b, TILE))))
+            keep_sums(way * tiles + k, masked_sums(taps, 0, fields), 0)
+
+    def gather_plane_close(way):
+        x = (0, nx - 1)[way]
+        for k in range(tiles):
+            row, at = own_tile(x, k)
+            for f in range(nspec):
+                qbuf[f, pl.ds(row, TILE), :] = qbuf[f, pl.ds(row, TILE), :] + merged(way * tiles + k, f, False)
+            own = pl.ds(at, TILE)
+            gathered[own, :] = gathered[own, :] + merged(way * tiles + k, flux, False)
+
+    def gather_ends(g):
+        for k, x, y in members:
+            row, at = own_tile(g * quad + x, y)
+            value = edge[pl.ds(at, TILE), :]
+            parts_e[k] = packed_taps(row, 1, lambda near: value, packed, 0)
+
+    def quotas(g):
+        for k, x, y in members:
+            row, at = own_tile(g * quad + x, y)
+            value = parts_e[k]
+
+            def spread(f):
+                return jnp.where(both_ends, pltpu.roll(value, LANES - 1 - 2 * f, 1), 0.0)
+
+            inverted = 1.0 / (gathered[pl.ds(at, TILE), :] + spread(flux))
+            for f in range(nspec):
+                qbuf[f, pl.ds(row, TILE), :] = (qbuf[f, pl.ds(row, TILE), :] + spread(f)) * inverted
+
+    def quota_pack(g):
+        for k, x, y in members:
+            row, at = own_tile(g * quad + x, y)
+            zs_f[1, pl.ds(at, TILE), :] = pack([qbuf[f, pl.ds(row, TILE), :] for f in range(nspec)], 0)
+
+    def scatter_main(t):
+        row, at = own_tile(t // tiles, t % tiles) if isinstance(t, int) else own_row(t)
+        taps = []
+        for a, b, position in BLOCK:
+            near = pl.ds(row - a * pitch - b, TILE)
+            source = codes[0, near, :]
+            center = None if position == 12 else source
+            taps.append(((source, center, source), position, reader(qbuf, near)))
+        keep_sums(0, masked_sums(taps, 0, nspec), 0)
+
+    def scatter_close(t):
+        row, at = own_tile(t // tiles, t % tiles) if isinstance(t, int) else own_row(t)
+        for f in range(nspec):
+            out[f, pl.ds(at, TILE), :] = merged(0, f, True)
+
+    def scatter_strip(j):
+        x = j * TILE
+        for way, (b, y) in enumerate(((1, -1), (-1, ny))):
+            taps = []
+            for a in (-1, 0, 1):
+                source = codes[0, pl.ds(first(1) + (x - a) * pitch + y, TILE, stride=pitch), :]
+                taps.append(((source, source, source), 9 * (a + 1) + 3 * (b + 1), reader(yr.at[1, way], pl.ds(TILE + x - a, TILE))))
+            keep_sums(way, masked_sums(taps, 0, nspec), 0)
+
+    def scatter_strip_close(j):
+        for way, y in enumerate((0, ny - 1)):
+            where = pl.ds(j * TILE * ny + y, TILE, stride=ny)
+            for f in range(nspec):
+                out[f, where, :] = out[f, where, :] + merged(way, f, True)
+
+    def scatter_plane(way):
+        a, x = ((1, 0), (-1, nx + 1))[way]
+        for k in range(tiles):
+            taps = []
+            for b in (-1, 0, 1):
+                source = codes[0, pl.ds(first(x) + k * TILE - b, TILE), :]
+                taps.append(((source, source, source), 9 * (a + 1) + 3 * (b + 1), reader(xr.at[1, way], pl.ds(TILE + k * TILE - b, TILE))))
+            keep_sums(way * tiles + k, masked_sums(taps, 0, nspec), 0)
+
+    def scatter_plane_close(way):
+        x = (0, nx - 1)[way]
+        for k in range(tiles):
+            row, at = own_tile(x, k)
+            for f in range(nspec):
+                out[f, pl.ds(at, TILE), :] = out[f, pl.ds(at, TILE), :] + merged(way * tiles + k, f, True)
+
+    def scatter_ends(g):
+        for k, x, y in members:
+            row, at = own_tile(g * quad + x, y)
+            parts_e[k] = packed_taps(row, -1, lambda near: codes[1, near, :], packed, 1)
+
+    def finals(g):
+        for k, x, y in members:
+            row, at = own_tile(g * quad + x, y)
+            own = pl.ds(at, TILE)
+            value, factor = parts_e[k], scaling[own, :]
+            for f in range(nspec):
+                spread = jnp.where(both_ends, pltpu.roll(value, LANES - 1 - 2 * f, 1), 0.0)
+                out[f, own, :] = factor * (out[f, own, :] + spread)
 
     blank(codes, 0, 2)
-    blank(wbuf, 0, fields + 1)
-    blank(qbuf, 0, nspec + 2)
+    blank(packed, 0, 2)
+    w_all.blank()
+    q_all.blank()
     loads[0].wait()
     loads[1].wait()
     lax.fori_loop(0, nx, fill, 0, unroll=8)
@@ -510,39 +674,39 @@
     code_packed.receive()
     pipelined([count_taps, weigh, weigh_pack], nx // quad)
     w_z.start()
-    w_a.start()
-    w_b.start()
-    reduce_start("gy", reduce_finish("gx"))
-    w_z.receive()
-    w_packed.start()
-    w_a.receive()
+    w_all.start()
+
+    def relay_w():
+        w_z.receive()
+        w_packed.start()
+        reduce_start("gy", reduce_finish("gx"))
+
+    pipelined([gather_main, gather_close], nx * tiles, (nx * tiles // 3, relay_w))
+    w_all.receive()
     w_packed.receive()
-    pipelined(quota_stages(0, cut + 1, True), nx)
-    qa_z.start()
-    q_a.start()
-    w_b.receive()
+    pipelined([gather_strip, gather_strip_close], nx // TILE)
+    for stage in (gather_plane, gather_plane_close):
+        stage(0)
+        stage(1)
+    pipelined([gather_ends, quotas, quota_pack], nx // quad)
+    q_z.start()
+    q_all.start()
     reduce_start("gz", reduce_finish("gy"))
 
-    def middle_a():
-        qa_z.receive()
-        qa_packed.start()
-
-    pipelined(quota_stages(cut + 1, fields, False), nx, (nx // 3, middle_a))
-    qb_z.start()
-    q_b.start()
-    summed = reduce_finish("gz")
-    change[...] = jnp.broadcast_to(jnp.sum(summed, axis=1, keepdims=True) * scale, change.shape)
-    q_a.receive()
-    qa_packed.receive()
-
-    def middle_b():
-        qb_z.receive()
-        qb_packed.start()
-
-    pipelined(scatter_stages(group_a, nspec), nx, (nx // 3, middle_b))
-    q_b.receive()
-    qb_packed.receive()
-    pipelined(scatter_stages(group_b, nspec + 1), nx)
+    def relay_q():
+        q_z.receive()
+        q_packed.start()
+        summed = reduce_finish("gz")
+        change[...] = jnp.broadcast_to(jnp.sum(summed, axis=1, keepdims=True) * scale, change.shape)
+
+    pipelined([scatter_main, scatter_close], nx * tiles, (nx * tiles // 3, relay_q))
+    q_all.receive()
+    q_packed.receive()
+    pipelined([scatter_strip, scatter_strip_close], nx // TILE)
+    for stage in (scatter_plane, scatter_plane_close):
+        stage(0)
+        stage(1)
+    pipelined([scatter_ends, finals], nx // quad)
     for part in everything:
         part.finish()
 
@@ -552,28 +716,27 @@
     assert nz == LANES and ny % TILE == 0 and nx % TILE == 0
     own = nx * ny
     tiles = ny // TILE
-    rows = TILE + (nx + 2) * (ny + TILE)
+    rows = 2 * TILE + (nx + 2) * (ny + TILE)
     most = max(lax.axis_size(axis) for axis in AXES)
     cells = own * nz * math.prod(lax.axis_size(axis) for axis in AXES)
     high = -(-nspec // TILE) * TILE
-    cut = nspec // 2
     fields = nspec + 1
-    group = max(cut + 1, nspec - cut)
-    wide = -(-group // TILE) * TILE
+    wide = -(-fields // TILE) * TILE
     f32, i32 = jnp.float32, jnp.int32
     vmem = pl.BlockSpec(memory_space=pltpu.VMEM)
     hbm = pl.BlockSpec(memory_space=pltpu.HBM)
     shapes = [
         ((nspec, own, nz), f32), ((own, nz), i32), ((own, nz), i32), ((own, nz), i32), ((own, nz), i32),
-        ((2, rows, nz), i32), ((fields + 1, rows, nz), f32), ((nspec + 2, rows, nz), f32),
+        ((2, rows, nz), i32), ((fields, rows, nz), f32), ((nspec, rows, nz), f32), ((2, rows, nz), f32),
         ((2, own, nz), i32), ((own, nz), i32),
         ((own, nz), i32), ((own, nz), i32), ((own, nz), i32),
-        ((3, own, nz), f32), ((3, own, nz), f32), ((3, own, nz), f32),
+        ((2, own, nz), f32), ((2, own, nz), f32), ((2, own, nz), f32),
         ((2, 2, nx, nz), i32), ((2, 2, nx, nz), i32), ((2, 4, TILE, nz), i32), ((2, 4, TILE, nz), i32),
-        ((2, fields + 1, nx, nz), f32), ((2, fields + 1, nx, nz), f32), ((3, 4, wide, nz), f32), ((3, 4, wide, nz), f32),
-        ((2, nspec + 2, nx, nz), f32), ((2, nspec + 2, nx, nz), f32), ((4, 4, wide, nz), f32), ((4, 4, wide, nz), f32),
-        ((own, nz), f32), ((own, nz), f32), ((own, nz), f32),
-        ((2 * tiles, 4, TILE, nz), i32), ((tiles, 3, group + 1, TILE, nz), f32),
+        ((2, 2, nx, nz), f32), ((2, 2, nx, nz), f32), ((2, 4, TILE, nz), f32), ((2, 4, TILE, nz), f32),
+        ((2, 2, fields, ny + 2 * TILE, nz), f32), ((2, 2, fields, nx, nz), f32),
+        ((2, 2, fields, nx + 2 * TILE, nz), f32), ((2, 4, wide, nz), f32), ((2, 4, wide, nz), f32),
+        ((own, nz), f32), ((own, nz), f32),
+        ((2 * tiles, 4, TILE, nz), i32), ((2 * tiles, 3, fields, TILE, nz), f32), ((2 * tiles, TILE, nz), f32),
         ((3, most, high, nz), f32),
     ]
     dma = pltpu.SemaphoreType.DMA
@@ -587,7 +750,7 @@
         out_specs=(vmem, vmem),
         scratch_shapes=[pltpu.VMEM(shape, kind) for shape, kind in shapes]
         + [
-            dma((5,)), dma((4, 2)), dma((4, 2)), dma((9, 8)), dma((9, 8)), dma((3, most)), dma((3, most)),
+            dma((5,)), dma((3, 2)), dma((3, 2)), dma((6, 8)), dma((6, 8)), dma((3, most)), dma((3, most)),
         ],
         compiler_params=pltpu.CompilerParams(
             collective_id=0, has_side_effects=True, vmem_limit_bytes=26 * 1024 * 1024

time: 44.6 us -> 38.4 us (0.86)
  Pallas kernels: 41.8 us -> 35.6 us
    pallas_call x1, Pallas kernels: 41.8 us -> 35.6 us  [per_device(): pl.pallas_call(functools.partial(kernel, nx, ny, 1.0 / math.sqrt(cells)),...]
where the time goes in v3:
time: 38.4 us; the launch traced here: 38.3 us
  Pallas kernels  35.6 us (93%)
  local copies, waits for them, and re-layouts  2.03 us (5%)
  between operations  0.64 us (2%)
    pallas_call x1, Pallas kernels, per_device(): pl.pallas_call(functools.partial(kernel, nx, ny, 1.0 / math.sqrt(cells)),...  35.6 us
    unnamed x1, local copies, waits for them, and re-layouts  1.4 us

profile of v3, /device:TPU:0, one launch (start us, length us, event | category | flops | bytes accessed | tf_op | source)
XLA Modules:
  0.0 38.3 jit_solution(16598057563629433152)
XLA Ops:
  0.6 35.6 %shard_map.68 = (f32[9,512,128]{2,1,0:T(8,128)S(1)}, f32[16,128]{1,0:T(8,128)S(1)}) custom-call(f32[9,512,128]{2,1,0:T(8,128)} %bitcast.7, s32[512,128]{1,0:T(8,128)} %bitcast.8, s32[512,128]{1,0:T(8,128)} %bitcast.9, s32[512,128]{1,0:T(8,128)} %bitcast.10, s32[512,128]{1,0:T(8,128)} %bitcast.11), custom_call_target="tpu_custom_call" | custom-call | tf_op jit(solution)/shard_map/pallas_call | solution.py:743
  36.2 0.6 %slice_reduce_fusion = f32[9]{0:T(128)} fusion(f32[16,128]{1,0:T(8,128)S(1)} %get-tuple-element.5), kind=kLoop, calls=%fused_computation | loop fusion | bytes 72 | tf_op jit(solution)/shard_map/slice | solution.py:766
  36.9 1.4 %copy.8 = f32[9,32,16,128]{3,2,1,0:T(8,128)} copy(f32[9,32,16,128]{3,2,1,0:T(8,128)S(1)} %bitcast.6) | data formatting | bytes 4718592

commit v4 on v3

--- a/solution.py
+++ b/solution.py
@@ -46,15 +46,15 @@
     nx, ny, scale,
     prov_h, flag_h, code_h, vol_h, area_h,
     out, change,
-    prov, flag, code, vol, area,
+    raw, flag, code, vol, area,
     codes, wbuf, qbuf, packed, shifted, edge,
-    zs_i, zl_i, zr_i, zs_f, zl_f, zr_f,
+    zl_i, zr_i, zs_f, zl_f, zr_f,
     ys_i, yr_i, cs_i, cr_i, ys_p, yr_p, cs_p, cr_p,
-    xr, ys, yr, cs, cr,
-    gathered, scaling, parts_i, parts_f, parts_e, peers,
+    xr_r, ys_r, yr_r, cs_r, cr_r, xr_w, ys_w, yr_w, cs_w, cr_w, xr_q, ys_q, yr_q, cs_q, cr_q,
+    volumes, weights, gathered, scaling, parts_i, parts_f, parts_e, peers,
     load, z_send, z_recv, send, recv, peer_send, peer_recv,
 ):
-    nspec = prov.shape[0]
+    nspec = prov_h.shape[0]
     pitch = ny + TILE
     tiles = ny // TILE
     here = {axis: lax.axis_index(axis) for axis in AXES}
@@ -67,7 +67,7 @@
     fields = nspec + 1
     flux = nspec
 
-    inputs = [(flag_h, flag), (code_h, code), (vol_h, vol), (area_h, area), (prov_h, prov)]
+    inputs = [(flag_h, flag), (code_h, code), (vol_h, vol), (area_h, area), (prov_h, raw.at[pl.ds(0, nspec)])]
     loads = [pltpu.make_async_copy(src, dst, load.at[k]) for k, (src, dst) in enumerate(inputs)]
     for copy in loads:
         copy.start()
@@ -76,19 +76,13 @@
         return lax.rem(here[axis] + (step + size[axis]), size[axis])
 
     barrier = pltpu.get_barrier_semaphore()
-    others = set()
-    for dx, dy in WAYS:
-        others.add((dx % size["gx"], dy % size["gy"], 0))
-    for number, axis in enumerate(AXES):
-        for k in range(1, size[axis]):
-            others.add(tuple(k if i == number else 0 for i in range(3)))
-    others.discard((0, 0, 0))
-    for shift in sorted(others):
-        pl.semaphore_signal(
-            barrier, inc=1,
-            device_id={axis: lax.rem(here[axis] + shift[i], size[axis]) for i, axis in enumerate(AXES)},
-            device_id_type=MESH,
-        )
+    near_x = lax.min(here["gx"], 1) + lax.min(size["gx"] - 1 - here["gx"], 1)
+    near_y = lax.min(here["gy"], 1) + lax.min(size["gy"] - 1 - here["gy"], 1)
+    near_z = lax.min(here["gz"], 1) + lax.min(size["gz"] - 1 - here["gz"], 1)
+    greeted = (near_x + 1) * (near_y + 1) - 1 + near_z
+
+    def greet(target):
+        pl.semaphore_signal(barrier, inc=1, device_id=target, device_id_type=MESH)
 
     def first(x):
         return TILE + x * pitch
@@ -112,6 +106,10 @@
         return found
 
     below_z, above_z = side("gz", -1), side("gz", 1)
+    for dx, dy in WAYS:
+        pl.when(exists(dx, dy))(functools.partial(greet, {"gx": moved("gx", dx), "gy": moved("gy", dy)}))
+    pl.when(below_z)(functools.partial(greet, {"gz": moved("gz", -1)}))
+    pl.when(above_z)(functools.partial(greet, {"gz": moved("gz", 1)}))
 
     def edge_row(step):
         return ny - 1 if step > 0 else 0
@@ -245,8 +243,8 @@
             def place(x, carry):
                 for k in range(tiles):
                     row, at = own_tile(x, k)
-                    low = jnp.where(below_z, self.zl[pl.ds(at, TILE), :], zero)
-                    high = jnp.where(above_z, self.zr[pl.ds(at, TILE), :], zero)
+                    low = jnp.where(below_z, pltpu.roll(self.zl[pl.ds(at, TILE), :], 1, 1), zero)
+                    high = jnp.where(above_z, pltpu.roll(self.zr[pl.ds(at, TILE), :], LANES - 1, 1), zero)
                     self.buf[self.plane, pl.ds(row, TILE), :] = jnp.where(odd, low, high)
                 return carry
 
@@ -257,36 +255,31 @@
             pl.when(below_z)(self.copies[1].wait_send)
 
     class Faces:
-        def __init__(self, number, buf, n, which):
-            self.buf, self.n = buf, n
-            self.xr, self.ys, self.yr, self.cs, self.cr = xr.at[which], ys.at[which], yr.at[which], cs.at[which], cr.at[which]
+        def __init__(self, number, buf, n, start, step, landing):
+            self.buf, self.n, self.first_row, self.step = buf, n, start, step
+            self.xr, self.ys, self.yr, self.cs, self.cr = landing
             self.copies = []
             for k, (dx, dy) in enumerate(WAYS):
                 way = 0 if dx + dy > 0 else 1
                 if dy == 0:
-                    source = buf.at[pl.ds(0, n), pl.ds(first(nx if dx > 0 else 1), ny), :]
-                    landing = self.xr.at[way, pl.ds(0, n), pl.ds(TILE, ny), :]
+                    source = buf.at[pl.ds(0, n), pl.ds(start + (nx - 1 if dx > 0 else 0) * step, ny), :]
+                    target = self.xr.at[way, pl.ds(0, n), pl.ds(TILE, ny), :]
                 elif dx == 0:
-                    source = self.ys.at[way, pl.ds(0, n)]
-                    landing = self.yr.at[way, pl.ds(0, n), pl.ds(TILE, nx), :]
+                    source, target = self.ys.at[way], self.yr.at[way, pl.ds(0, n), pl.ds(TILE, nx), :]
                 else:
-                    source, landing = self.cs.at[k - 4], self.cr.at[k - 4]
+                    source, target = self.cs.at[k - 4], self.cr.at[k - 4]
                 self.copies.append(
                     pltpu.make_async_remote_copy(
-                        src_ref=source, dst_ref=landing,
+                        src_ref=source, dst_ref=target,
                         send_sem=send.at[number, k], recv_sem=recv.at[number, k],
                         device_id={"gx": moved("gx", dx), "gy": moved("gy", dy)}, device_id_type=MESH,
                     )
                 )
 
         def blank(self):
-            def low(f, carry):
-                zeros = jnp.zeros((TILE, LANES), jnp.float32)
-                for p in range(nx + 3):
-                    self.buf[f, pl.ds(p * pitch, TILE), :] = zeros
-                for p in (0, nx + 1):
-                    for k in range(tiles):
-                        self.buf[f, pl.ds(first(p) + k * TILE, TILE), :] = zeros
+            zeros = jnp.zeros((TILE, LANES), jnp.float32)
+
+            def borders(f, carry):
                 for way in range(2):
                     for at in (0, TILE + ny):
                         self.xr[way, f, pl.ds(at, TILE), :] = zeros
@@ -294,7 +287,7 @@
                         self.yr[way, f, pl.ds(at, TILE), :] = zeros
                 return carry
 
-            lax.fori_loop(0, self.n, low, 0)
+            lax.fori_loop(0, self.n, borders, 0)
 
             def clear(ref, way, extent):
                 def body(f, carry):
@@ -307,14 +300,15 @@
                 pl.when(jnp.logical_not(exists(0, -step)))(functools.partial(clear, self.yr, way, nx))
 
         def start(self):
-            buf = self.buf
+            buf, step = self.buf, self.step
 
             def gather(f, carry):
                 for x in range(0, nx, TILE):
-                    for way, step in ((0, 1), (1, -1)):
-                        self.ys[way, f, pl.ds(x, TILE), :] = buf[f, pl.ds(first(x + 1) + edge_row(step), TILE, stride=pitch), :]
+                    for way, toward in ((0, 1), (1, -1)):
+                        row = self.first_row + x * step + edge_row(toward)
+                        self.ys[way, f, pl.ds(x, TILE), :] = buf[f, pl.ds(row, TILE, stride=step), :]
                 for k, (dx, dy) in enumerate(WAYS[4:]):
-                    row = first(nx if dx > 0 else 1) + edge_row(dy)
+                    row = self.first_row + (nx - 1 if dx > 0 else 0) * step + edge_row(dy)
                     self.cs[k, pl.ds(f, 1), :] = buf[f, pl.ds(row, 1), :]
                 return carry
 
@@ -344,41 +338,62 @@
             for k, (dx, dy) in enumerate(WAYS):
                 pl.when(exists(dx, dy))(self.copies[k].wait_send)
 
-    code_z = Depth(0, zs_i, zl_i, zr_i, codes, 1)
+    def pad_zeros(buf, n):
+        zeros = jnp.zeros((TILE, LANES), jnp.float32)
+
+        def body(f, carry):
+            for p in range(nx + 3):
+                buf[f, pl.ds(p * pitch, TILE), :] = zeros
+            for p in (0, nx + 1):
+                for k in range(tiles):
+                    buf[f, pl.ds(first(p) + k * TILE, TILE), :] = zeros
+            return carry
+
+        lax.fori_loop(0, n, body, 0)
+
+    code_z = Depth(0, edge, zl_i, zr_i, codes, 1)
     code_own = Unit(0, codes, 0, 1, ys_i, yr_i, cs_i, cr_i, 0)
     code_packed = Unit(1, codes, 1, 2, ys_i, yr_i, cs_i, cr_i, 1)
-    w_z = Depth(1, zs_f.at[0], zl_f.at[0], zr_f.at[0], packed, 0)
-    w_all = Faces(2, wbuf, fields, 0)
-    w_packed = Unit(3, packed, 0, 1, ys_p, yr_p, cs_p, cr_p, 0)
-    q_z = Depth(2, zs_f.at[1], zl_f.at[1], zr_f.at[1], packed, 1)
-    q_all = Faces(4, qbuf, nspec, 1)
-    q_packed = Unit(5, packed, 1, 2, ys_p, yr_p, cs_p, cr_p, 1)
-    everything = [code_z, code_own, code_packed, w_z, w_all, w_packed, q_z, q_all, q_packed]
-
-    def peer_copies(axis):
-        number = AXES.index(axis)
-        return [
-            pltpu.make_async_remote_copy(
-                src_ref=peers.at[number, here[axis]], dst_ref=peers.at[number, here[axis]],
-                send_sem=peer_send.at[number, k], recv_sem=peer_recv.at[number, k],
-                device_id={axis: lax.rem(here[axis] + k, size[axis])}, device_id_type=MESH,
-            )
-            for k in range(1, size[axis])
-        ]
-
-    def reduce_start(axis, value):
-        peers[AXES.index(axis), here[axis]] = value
-        for copy in peer_copies(axis):
-            copy.start()
-
-    def reduce_finish(axis):
-        number = AXES.index(axis)
-        for copy in peer_copies(axis):
-            copy.wait()
-        value = peers[number, 0]
-        for k in range(1, size[axis]):
-            value = value + peers[number, k]
-        return value
+    raw_z = Depth(1, zs_f.at[0], zl_f.at[0], zr_f.at[0], packed, 0)
+    raw_all = Faces(2, raw, fields, 0, ny, (xr_r, ys_r, yr_r, cs_r, cr_r))
+    raw_packed = Unit(3, packed, 0, 1, ys_p, yr_p, cs_p, cr_p, 0)
+    w_z = Depth(2, zs_f.at[1], zl_f.at[1], zr_f.at[1], packed, 1)
+    w_all = Faces(4, weights, 1, 0, ny, (xr_w, ys_w, yr_w, cs_w, cr_w))
+    w_packed = Unit(5, packed, 1, 2, ys_p, yr_p, cs_p, cr_p, 1)
+    q_z = Depth(3, zs_f.at[2], zl_f.at[2], zr_f.at[2], packed, 2)
+    q_all = Faces(6, qbuf, nspec, first(1), pitch, (xr_q, ys_q, yr_q, cs_q, cr_q))
+    q_packed = Unit(7, packed, 2, 3, ys_p, yr_p, cs_p, cr_p, 2)
+    everything = [
+        code_z, code_own, code_packed, raw_z, raw_all, raw_packed, w_z, w_all, w_packed, q_z, q_all, q_packed,
+    ]
+
+    def total_over(value):
+        for number, axis in enumerate(AXES):
+            n, me = size[axis], here[axis]
+            peers[number, me] = value
+            for k in range(1, n):
+                def copy(way, slot):
+                    block = peers.at[number, lax.max(lax.min(slot, n - 1), 0)]
+                    return pltpu.make_async_remote_copy(
+                        src_ref=block, dst_ref=block,
+                        send_sem=peer_send.at[number, k, way], recv_sem=peer_recv.at[number, k, way],
+                        device_id={axis: moved(axis, 1 if way == 0 else -1)}, device_id_type=MESH,
+                    )
+
+                up, down = me - k + 1, me + k - 1
+                sends = [(jnp.logical_and(up >= 0, me < n - 1), copy(0, up)), (jnp.logical_and(down < n, me > 0), copy(1, down))]
+                lands = [(me - k >= 0, copy(0, me - k)), (me + k < n, copy(1, me + k))]
+                for there, block in sends:
+                    pl.when(there)(block.start)
+                yield
+                for there, block in lands:
+                    pl.when(there)(block.wait_recv)
+                for there, block in sends:
+                    pl.when(there)(block.wait_send)
+            value = peers[number, 0]
+            for k in range(1, n):
+                value = value + peers[number, k]
+        change[...] = jnp.broadcast_to(jnp.sum(value, axis=1, keepdims=True) * scale, change.shape)
 
     def fractions(own):
         is_cut = flag[own, :] == 1
@@ -392,21 +407,36 @@
             own = pl.ds(at, TILE)
             value = jnp.where(flag[own, :] == 1, code[own, :] | CENTER, CENTER)
             codes[0, pl.ds(row, TILE), :] = value
+            low = jnp.broadcast_to(value[:, :1], (TILE, LANES))
+            high = lax.shift_right_logical(jnp.broadcast_to(value[:, LANES - 1:], (TILE, LANES)), 2)
+            edge[own, :] = jnp.where(odd, low, high)
+        return carry
+
+    def shift(x, carry):
+        for k in range(tiles):
+            row, at = own_tile(x, k)
+            own = pl.ds(at, TILE)
+            value = codes[0, pl.ds(row, TILE), :]
             shifted[0, own, :] = jnp.where(first_lane, 0, pltpu.roll(value, 1, 1))
             shifted[1, own, :] = jnp.where(last_lane, 0, pltpu.roll(value, LANES - 1, 1))
-            low = jnp.broadcast_to(value[:, :1], (TILE, LANES))
-            high = lax.shift_right_logical(jnp.broadcast_to(value[:, LANES - 1:], (TILE, LANES)), 2)
-            zs_i[own, :] = jnp.where(odd, high, low)
-            edge[own, :] = jnp.where(odd, low, high)
         return carry
 
-    def add_up(x, totals):
+    def prepare(x, totals):
         for k in range(tiles):
             _, at = own_tile(x, k)
             own = pl.ds(at, TILE)
-            volume, _ = fractions(own)
-            totals = tuple(totals[s] + volume * prov[s, own, :] for s in range(nspec))
+            volume, face = fractions(own)
+            volumes[own, :] = volume
+            raw[nspec, own, :] = face
+            totals = tuple(totals[s] + volume * raw[s, own, :] for s in range(nspec))
         return totals
+
+    def raw_pack(x, carry):
+        for k in range(tiles):
+            _, at = own_tile(x, k)
+            own = pl.ds(at, TILE)
+            zs_f[0, own, :] = pack([raw[f, own, :] for f in range(fields)], 0)
+        return carry
 
     def masked_sums(taps, low, high):
         zero = jnp.zeros((TILE, LANES), jnp.float32)
@@ -436,12 +466,12 @@
             up, down = pltpu.roll(parts_f[slot, 2, f], LANES - 1, 1), pltpu.roll(parts_f[slot, 0, f], 1, 1)
         return parts_f[slot, 1, f] + up + down
 
-    def packed_taps(row, step, source, buf, plane):
+    def packed_taps(row, step, source, value_of):
         zero = jnp.zeros((TILE, LANES), jnp.float32)
         total = None
         for a, b, position in BLOCK:
             near = pl.ds(row + step * (a * pitch + b), TILE)
-            term = jnp.where((source(near) & (1 << position)) != 0, buf[plane, near, :], zero)
+            term = jnp.where((source(near) & (1 << position)) != 0, value_of(near), zero)
             total = term if total is None else total + term
         return total
 
@@ -449,9 +479,7 @@
         packed = jnp.zeros((TILE, LANES), jnp.float32)
         for k, value in enumerate(values):
             f = lowest + k
-            start = value if f == 0 else pltpu.roll(value, 2 * f, 1)
-            packed = jnp.where(lane == 2 * f, start, packed)
-            packed = jnp.where(lane == 2 * f + 1, pltpu.roll(value, 2 * f + 2, 1), packed)
+            packed = jnp.where((lane == 2 * f) | (lane == 2 * f + 1), pltpu.roll(value, 2 * f + 1, 1), packed)
         return packed
 
     quad = 2
@@ -485,18 +513,21 @@
             from_right = pltpu.roll(parts_i[k, 0], LANES - 1, 1)
             counted = lax.shift_right_logical(parts_i[k, 1], 1)
             counted = counted + jnp.where(first_lane, from_end, from_left) + jnp.where(last_lane, from_end, from_right)
-            volume, face = fractions(own)
             share = 1.0 / counted.astype(jnp.float32)
-            scaling[own, :] = face * share
-            weight = volume * share
-            for s in range(nspec):
-                wbuf[s, pl.ds(row, TILE), :] = weight * prov[s, own, :]
-            wbuf[flux, pl.ds(row, TILE), :] = weight * face
+            scaling[own, :] = raw[nspec, own, :] * share
+            weight = volumes[own, :] * share
+            weights[0, own, :] = weight
+            for f in range(fields):
+                wbuf[f, pl.ds(row, TILE), :] = weight * raw[f, own, :]
 
     def weigh_pack(g):
         for k, x, y in members:
             row, at = own_tile(g * quad + x, y)
-            zs_f[0, pl.ds(at, TILE), :] = pack([wbuf[f, pl.ds(row, TILE), :] for f in range(fields)], 0)
+            own = pl.ds(at, TILE)
+            value = weights[0, own, :]
+            low = jnp.broadcast_to(value[:, :1], (TILE, LANES))
+            high = jnp.broadcast_to(value[:, LANES - 1:], (TILE, LANES))
+            zs_f[1, own, :] = jnp.where(odd, low, high)
 
     def own_row(t):
         x, k = lax.div(t, tiles), lax.rem(t, tiles)
@@ -507,6 +538,10 @@
 
     def reader(buf, near):
         return lambda f: buf[f, near, :]
+
+    def weighed(buf, factors, near):
+        factor = factors[0, near, :]
+        return lambda f: buf[f, near, :] * factor
 
     def gather_main(t):
         row, at = own_tile(t // tiles, t % tiles) if isinstance(t, int) else own_row(t)
@@ -532,7 +567,8 @@
             middle = codes[0, pl.ds(first(1) + x * pitch + y, TILE, stride=pitch), :]
             taps = []
             for a in (-1, 0, 1):
-                taps.append(((left, middle, right), 9 * (a + 1) + 3 * (b + 1), reader(yr.at[0, way], pl.ds(TILE + x + a, TILE))))
+                near = pl.ds(TILE + x + a, TILE)
+                taps.append(((left, middle, right), 9 * (a + 1) + 3 * (b + 1), weighed(yr_r.at[way], yr_w.at[way], near)))
             keep_sums(way, masked_sums(taps, 0, fields), 0)
 
     def gather_strip_close(j):
@@ -552,7 +588,8 @@
             right, left, middle = shifted[0, own, :], shifted[1, own, :], codes[0, pl.ds(row, TILE), :]
             taps = []
             for b in (-1, 0, 1):
-                taps.append(((left, middle, right), 9 * (a + 1) + 3 * (b + 1), reader(xr.at[0, way], pl.ds(TILE + k * TILE + b, TILE))))
+                near = pl.ds(TILE + k * TILE + b, TILE)
+                taps.append(((left, middle, right), 9 * (a + 1) + 3 * (b + 1), weighed(xr_r.at[way], xr_w.at[way], near)))
             keep_sums(way * tiles + k, masked_sums(taps, 0, fields), 0)
 
     def gather_plane_close(way):
@@ -568,7 +605,8 @@
         for k, x, y in members:
             row, at = own_tile(g * quad + x, y)
             value = edge[pl.ds(at, TILE), :]
-            parts_e[k] = packed_taps(row, 1, lambda near: value, packed, 0)
+            parts_e[k] = packed_taps(
+                row, 1, lambda near: value, lambda near: packed[0, near, :] * packed[1, near, :])
 
     def quotas(g):
         for k, x, y in members:
@@ -585,7 +623,7 @@
     def quota_pack(g):
         for k, x, y in members:
             row, at = own_tile(g * quad + x, y)
-            zs_f[1, pl.ds(at, TILE), :] = pack([qbuf[f, pl.ds(row, TILE), :] for f in range(nspec)], 0)
+            zs_f[2, pl.ds(at, TILE), :] = pack([qbuf[f, pl.ds(row, TILE), :] for f in range(nspec)], 0)
 
     def scatter_main(t):
         row, at = own_tile(t // tiles, t % tiles) if isinstance(t, int) else own_row(t)
@@ -608,7 +646,7 @@
             taps = []
             for a in (-1, 0, 1):
                 source = codes[0, pl.ds(first(1) + (x - a) * pitch + y, TILE, stride=pitch), :]
-                taps.append(((source, source, source), 9 * (a + 1) + 3 * (b + 1), reader(yr.at[1, way], pl.ds(TILE + x - a, TILE))))
+                taps.append(((source, source, source), 9 * (a + 1) + 3 * (b + 1), reader(yr_q.at[way], pl.ds(TILE + x - a, TILE))))
             keep_sums(way, masked_sums(taps, 0, nspec), 0)
 
     def scatter_strip_close(j):
@@ -623,7 +661,7 @@
             taps = []
             for b in (-1, 0, 1):
                 source = codes[0, pl.ds(first(x) + k * TILE - b, TILE), :]
-                taps.append(((source, source, source), 9 * (a + 1) + 3 * (b + 1), reader(xr.at[1, way], pl.ds(TILE + k * TILE - b, TILE))))
+                taps.append(((source, source, source), 9 * (a + 1) + 3 * (b + 1), reader(xr_q.at[way], pl.ds(TILE + k * TILE - b, TILE))))
             keep_sums(way * tiles + k, masked_sums(taps, 0, nspec), 0)
 
     def scatter_plane_close(way):
@@ -636,7 +674,7 @@
     def scatter_ends(g):
         for k, x, y in members:
             row, at = own_tile(g * quad + x, y)
-            parts_e[k] = packed_taps(row, -1, lambda near: codes[1, near, :], packed, 1)
+            parts_e[k] = packed_taps(row, -1, lambda near: codes[1, near, :], lambda near: packed[2, near, :])
 
     def finals(g):
         for k, x, y in members:
@@ -648,42 +686,56 @@
                 out[f, own, :] = factor * (out[f, own, :] + spread)
 
     blank(codes, 0, 2)
-    blank(packed, 0, 2)
-    w_all.blank()
-    q_all.blank()
     loads[0].wait()
     loads[1].wait()
     lax.fori_loop(0, nx, fill, 0, unroll=8)
-    pl.semaphore_wait(barrier, len(others))
+    pl.semaphore_wait(barrier, greeted)
     code_z.start()
     code_own.start()
     for copy in loads[2:]:
         copy.wait()
     totals = tuple(jnp.zeros((TILE, LANES), jnp.float32) for _ in range(nspec))
-    totals = lax.fori_loop(0, nx // 2, add_up, totals, unroll=2)
-    code_z.receive()
-    code_packed.start()
-    totals = lax.fori_loop(nx // 2, nx, add_up, totals, unroll=2)
+    totals = lax.fori_loop(0, nx, prepare, totals, unroll=2)
     local = jnp.concatenate(
         [jnp.sum(total, axis=0, keepdims=True) for total in totals]
         + [jnp.zeros((peers.shape[2] - nspec, LANES), jnp.float32)],
         axis=0,
     )
-    reduce_start("gx", local)
+    reduction = total_over(local)
+    code_z.receive()
+    code_packed.start()
+    raw_all.start()
+    next(reduction, None)
+    lax.fori_loop(0, nx, raw_pack, 0, unroll=4)
+    raw_z.start()
+    lax.fori_loop(0, nx, shift, 0, unroll=8)
+    blank(packed, 0, 3)
+    raw_all.blank()
+    w_all.blank()
+    q_all.blank()
+    pad_zeros(wbuf, fields)
+    pad_zeros(qbuf, nspec)
     code_own.receive()
     code_packed.receive()
+    raw_z.receive()
+    raw_packed.start()
+    next(reduction, None)
     pipelined([count_taps, weigh, weigh_pack], nx // quad)
     w_z.start()
     w_all.start()
+    next(reduction, None)
 
     def relay_w():
         w_z.receive()
         w_packed.start()
-        reduce_start("gy", reduce_finish("gx"))
-
-    pipelined([gather_main, gather_close], nx * tiles, (nx * tiles // 3, relay_w))
+        next(reduction, None)
+
+    pipelined([gather_main, gather_close], nx * tiles, (nx * tiles // 4, relay_w))
+    raw_all.receive()
+    raw_packed.receive()
     w_all.receive()
     w_packed.receive()
+    next(reduction, None)
     pipelined([gather_strip, gather_strip_close], nx // TILE)
     for stage in (gather_plane, gather_plane_close):
         stage(0)
@@ -691,15 +743,16 @@
     pipelined([gather_ends, quotas, quota_pack], nx // quad)
     q_z.start()
     q_all.start()
-    reduce_start("gz", reduce_finish("gy"))
+    next(reduction, None)
 
     def relay_q():
         q_z.receive()
         q_packed.start()
-        summed = reduce_finish("gz")
-        change[...] = jnp.broadcast_to(jnp.sum(summed, axis=1, keepdims=True) * scale, change.shape)
-
-    pipelined([scatter_main, scatter_close], nx * tiles, (nx * tiles // 3, relay_q))
+        next(reduction, None)
+
+    pipelined([scatter_main, scatter_close], nx * tiles, (nx * tiles // 4, relay_q))
+    for _ in reduction:
+        pass
     q_all.receive()
     q_packed.receive()
     pipelined([scatter_strip, scatter_strip_close], nx // TILE)
@@ -719,23 +772,28 @@
     rows = 2 * TILE + (nx + 2) * (ny + TILE)
     most = max(lax.axis_size(axis) for axis in AXES)
     cells = own * nz * math.prod(lax.axis_size(axis) for axis in AXES)
-    high = -(-nspec // TILE) * TILE
     fields = nspec + 1
-    wide = -(-fields // TILE) * TILE
     f32, i32 = jnp.float32, jnp.int32
     vmem = pl.BlockSpec(memory_space=pltpu.VMEM)
     hbm = pl.BlockSpec(memory_space=pltpu.HBM)
     shapes = [
-        ((nspec, own, nz), f32), ((own, nz), i32), ((own, nz), i32), ((own, nz), i32), ((own, nz), i32),
-        ((2, rows, nz), i32), ((fields, rows, nz), f32), ((nspec, rows, nz), f32), ((2, rows, nz), f32),
+        ((fields, own, nz), f32), ((own, nz), i32), ((own, nz), i32), ((own, nz), i32), ((own, nz), i32),
+        ((2, rows, nz), i32), ((fields, rows, nz), f32), ((nspec, rows, nz), f32), ((3, rows, nz), f32),
         ((2, own, nz), i32), ((own, nz), i32),
-        ((own, nz), i32), ((own, nz), i32), ((own, nz), i32),
-        ((2, own, nz), f32), ((2, own, nz), f32), ((2, own, nz), f32),
+        ((own, nz), i32), ((own, nz), i32),
+        ((3, own, nz), f32), ((3, own, nz), f32), ((3, own, nz), f32),
         ((2, 2, nx, nz), i32), ((2, 2, nx, nz), i32), ((2, 4, TILE, nz), i32), ((2, 4, TILE, nz), i32),
-        ((2, 2, nx, nz), f32), ((2, 2, nx, nz), f32), ((2, 4, TILE, nz), f32), ((2, 4, TILE, nz), f32),
-        ((2, 2, fields, ny + 2 * TILE, nz), f32), ((2, 2, fields, nx, nz), f32),
-        ((2, 2, fields, nx + 2 * TILE, nz), f32), ((2, 4, wide, nz), f32), ((2, 4, wide, nz), f32),
-        ((own, nz), f32), ((own, nz), f32),
+        ((2, 3, nx, nz), f32), ((2, 3, nx, nz), f32), ((3, 4, TILE, nz), f32), ((3, 4, TILE, nz), f32),
+    ]
+    for n in (fields, 1, nspec):
+        high = -(-n // TILE) * TILE
+        shapes += [
+            ((2, n, ny + 2 * TILE, nz), f32), ((2, n, nx, nz), f32), ((2, n, nx + 2 * TILE, nz), f32),
+            ((4, high, nz), f32), ((4, high, nz), f32),
+        ]
+    high = -(-nspec // TILE) * TILE
+    shapes += [
+        ((own, nz), f32), ((1, own, nz), f32), ((own, nz), f32), ((own, nz), f32),
         ((2 * tiles, 4, TILE, nz), i32), ((2 * tiles, 3, fields, TILE, nz), f32), ((2 * tiles, TILE, nz), f32),
         ((3, most, high, nz), f32),
     ]
@@ -750,7 +808,7 @@
         out_specs=(vmem, vmem),
         scratch_shapes=[pltpu.VMEM(shape, kind) for shape, kind in shapes]
         + [
-            dma((5,)), dma((3, 2)), dma((3, 2)), dma((6, 8)), dma((6, 8)), dma((3, most)), dma((3, most)),
+            dma((5,)), dma((4, 2)), dma((4, 2)), dma((8, 8)), dma((8, 8)), dma((3, most, 2)), dma((3, most, 2)),
         ],
         compiler_params=pltpu.CompilerParams(
             collective_id=0, has_side_effects=True, vmem_limit_bytes=26 * 1024 * 1024

time: 38.4 us -> 45.1 us (1.17)
  Pallas kernels: 35.6 us -> 42.3 us
    pallas_call x1, Pallas kernels: 35.6 us -> 42.3 us  [per_device(): pl.pallas_call(functools.partial(kernel, nx, ny, 1.0 / math.sqrt(cells)),...]
where the time goes in v4:
time: 45.1 us; the launch traced here: 44.9 us
  Pallas kernels  42.3 us (94%)
  local copies, waits for them, and re-layouts  2.03 us (5%)
  between operations  0.64 us (1%)
    pallas_call x1, Pallas kernels, per_device(): pl.pallas_call(functools.partial(kernel, nx, ny, 1.0 / math.sqrt(cells)),...  42.3 us
    unnamed x1, local copies, waits for them, and re-layouts  1.4 us

profile of v4, /device:TPU:0, one launch (start us, length us, event | category | flops | bytes accessed | tf_op | source)
XLA Modules:
  0.0 44.9 jit_solution(10128328970722462546)
XLA Ops:
  0.6 42.3 %shard_map.68 = (f32[9,512,128]{2,1,0:T(8,128)S(1)}, f32[16,128]{1,0:T(8,128)S(1)}) custom-call(f32[9,512,128]{2,1,0:T(8,128)} %bitcast.7, s32[512,128]{1,0:T(8,128)} %bitcast.8, s32[512,128]{1,0:T(8,128)} %bitcast.9, s32[512,128]{1,0:T(8,128)} %bitcast.10, s32[512,128]{1,0:T(8,128)} %bitcast.11), custom_call_target="tpu_custom_call" | custom-call | tf_op jit(solution)/shard_map/pallas_call | solution.py:801
  42.9 0.6 %slice_reduce_fusion = f32[9]{0:T(128)} fusion(f32[16,128]{1,0:T(8,128)S(1)} %get-tuple-element.5), kind=kLoop, calls=%fused_computation | loop fusion | bytes 72 | tf_op jit(solution)/shard_map/slice | solution.py:824
  43.5 1.4 %copy.8 = f32[9,32,16,128]{3,2,1,0:T(8,128)} copy(f32[9,32,16,128]{3,2,1,0:T(8,128)S(1)} %bitcast.6) | data formatting | bytes 4718592

commit v5 on v4

--- a/solution.py
+++ b/solution.py
@@ -80,6 +80,9 @@
     near_y = lax.min(here["gy"], 1) + lax.min(size["gy"] - 1 - here["gy"], 1)
     near_z = lax.min(here["gz"], 1) + lax.min(size["gz"] - 1 - here["gz"], 1)
     greeted = (near_x + 1) * (near_y + 1) - 1 + near_z
+    for axis, near in (("gx", near_x), ("gy", near_y), ("gz", near_z)):
+        if size[axis] > 4:
+            greeted = greeted + (size[axis] - 1 - near)
 
     def greet(target):
         pl.semaphore_signal(barrier, inc=1, device_id=target, device_id_type=MESH)
@@ -110,6 +113,11 @@
         pl.when(exists(dx, dy))(functools.partial(greet, {"gx": moved("gx", dx), "gy": moved("gy", dy)}))
     pl.when(below_z)(functools.partial(greet, {"gz": moved("gz", -1)}))
     pl.when(above_z)(functools.partial(greet, {"gz": moved("gz", 1)}))
+    for axis in AXES:
+        if size[axis] > 4:
+            for k in range(2, size[axis]):
+                pl.when(here[axis] >= k)(functools.partial(greet, {axis: moved(axis, -k)}))
+                pl.when(here[axis] + k < size[axis])(functools.partial(greet, {axis: moved(axis, k)}))
 
     def edge_row(step):
         return ny - 1 if step > 0 else 0
@@ -371,25 +379,19 @@
         for number, axis in enumerate(AXES):
             n, me = size[axis], here[axis]
             peers[number, me] = value
-            for k in range(1, n):
-                def copy(way, slot):
-                    block = peers.at[number, lax.max(lax.min(slot, n - 1), 0)]
-                    return pltpu.make_async_remote_copy(
-                        src_ref=block, dst_ref=block,
-                        send_sem=peer_send.at[number, k, way], recv_sem=peer_recv.at[number, k, way],
-                        device_id={axis: moved(axis, 1 if way == 0 else -1)}, device_id_type=MESH,
-                    )
-
-                up, down = me - k + 1, me + k - 1
-                sends = [(jnp.logical_and(up >= 0, me < n - 1), copy(0, up)), (jnp.logical_and(down < n, me > 0), copy(1, down))]
-                lands = [(me - k >= 0, copy(0, me - k)), (me + k < n, copy(1, me + k))]
-                for there, block in sends:
-                    pl.when(there)(block.start)
-                yield
-                for there, block in lands:
-                    pl.when(there)(block.wait_recv)
-                for there, block in sends:
-                    pl.when(there)(block.wait_send)
+            copies = [
+                pltpu.make_async_remote_copy(
+                    src_ref=peers.at[number, me], dst_ref=peers.at[number, me],
+                    send_sem=peer_send.at[number, k], recv_sem=peer_recv.at[number, k],
+                    device_id={axis: lax.rem(me + k, n)}, device_id_type=MESH,
+                )
+                for k in range(1, n)
+            ]
+            for copy in copies:
+                copy.start()
+            yield
+            for copy in copies:
+                copy.wait()
             value = peers[number, 0]
             for k in range(1, n):
                 value = value + peers[number, k]
@@ -638,7 +640,7 @@
     def scatter_close(t):
         row, at = own_tile(t // tiles, t % tiles) if isinstance(t, int) else own_row(t)
         for f in range(nspec):
-            out[f, pl.ds(at, TILE), :] = merged(0, f, True)
+            wbuf[f, pl.ds(row, TILE), :] = merged(0, f, True)
 
     def scatter_strip(j):
         x = j * TILE
@@ -651,9 +653,9 @@
 
     def scatter_strip_close(j):
         for way, y in enumerate((0, ny - 1)):
-            where = pl.ds(j * TILE * ny + y, TILE, stride=ny)
+            where = pl.ds(first(1) + j * TILE * pitch + y, TILE, stride=pitch)
             for f in range(nspec):
-                out[f, where, :] = out[f, where, :] + merged(way, f, True)
+                wbuf[f, where, :] = wbuf[f, where, :] + merged(way, f, True)
 
     def scatter_plane(way):
         a, x = ((1, 0), (-1, nx + 1))[way]
@@ -669,7 +671,7 @@
         for k in range(tiles):
             row, at = own_tile(x, k)
             for f in range(nspec):
-                out[f, pl.ds(at, TILE), :] = out[f, pl.ds(at, TILE), :] + merged(way * tiles + k, f, True)
+                wbuf[f, pl.ds(row, TILE), :] = wbuf[f, pl.ds(row, TILE), :] + merged(way * tiles + k, f, True)
 
     def scatter_ends(g):
         for k, x, y in members:
@@ -683,7 +685,7 @@
             value, factor = parts_e[k], scaling[own, :]
             for f in range(nspec):
                 spread = jnp.where(both_ends, pltpu.roll(value, LANES - 1 - 2 * f, 1), 0.0)
-                out[f, own, :] = factor * (out[f, own, :] + spread)
+                out[f, own, :] = factor * (wbuf[f, pl.ds(row, TILE), :] + spread)
 
     blank(codes, 0, 2)
     loads[0].wait()
@@ -705,7 +707,6 @@
     code_z.receive()
     code_packed.start()
     raw_all.start()
-    next(reduction, None)
     lax.fori_loop(0, nx, raw_pack, 0, unroll=4)
     raw_z.start()
     lax.fori_loop(0, nx, shift, 0, unroll=8)
@@ -719,23 +720,20 @@
     code_packed.receive()
     raw_z.receive()
     raw_packed.start()
-    next(reduction, None)
     pipelined([count_taps, weigh, weigh_pack], nx // quad)
     w_z.start()
     w_all.start()
-    next(reduction, None)
 
     def relay_w():
         w_z.receive()
         w_packed.start()
-        next(reduction, None)
 
     pipelined([gather_main, gather_close], nx * tiles, (nx * tiles // 4, relay_w))
     raw_all.receive()
     raw_packed.receive()
     w_all.receive()
     w_packed.receive()
-    next(reduction, None)
+    next(reduction)
     pipelined([gather_strip, gather_strip_close], nx // TILE)
     for stage in (gather_plane, gather_plane_close):
         stage(0)
@@ -743,23 +741,22 @@
     pipelined([gather_ends, quotas, quota_pack], nx // quad)
     q_z.start()
     q_all.start()
-    next(reduction, None)
 
     def relay_q():
         q_z.receive()
         q_packed.start()
-        next(reduction, None)
+        next(reduction)
 
     pipelined([scatter_main, scatter_close], nx * tiles, (nx * tiles // 4, relay_q))
-    for _ in reduction:
-        pass
     q_all.receive()
     q_packed.receive()
+    next(reduction)
     pipelined([scatter_strip, scatter_strip_close], nx // TILE)
     for stage in (scatter_plane, scatter_plane_close):
         stage(0)
         stage(1)
     pipelined([scatter_ends, finals], nx // quad)
+    next(reduction, None)
     for part in everything:
         part.finish()
 
@@ -808,7 +805,7 @@
         out_specs=(vmem, vmem),
         scratch_shapes=[pltpu.VMEM(shape, kind) for shape, kind in shapes]
         + [
-            dma((5,)), dma((4, 2)), dma((4, 2)), dma((8, 8)), dma((8, 8)), dma((3, most, 2)), dma((3, most, 2)),
+            dma((5,)), dma((4, 2)), dma((4, 2)), dma((8, 8)), dma((8, 8)), dma((3, most)), dma((3, most)),
         ],
         compiler_params=pltpu.CompilerParams(
             collective_id=0, has_side_effects=True, vmem_limit_bytes=26 * 1024 * 1024

time: 45.1 us -> 36.5 us (0.81)
  Pallas kernels: 42.3 us -> 33.6 us
    pallas_call x1, Pallas kernels: 42.3 us -> 33.6 us  [per_device(): pl.pallas_call(functools.partial(kernel, nx, ny, 1.0 / math.sqrt(cells)),...]
where the time goes in v5:
time: 36.5 us; the launch traced here: 36.3 us
  Pallas kernels  33.6 us (92%)
  local copies, waits for them, and re-layouts  2.03 us (6%)
  between operations  0.64 us (2%)
    pallas_call x1, Pallas kernels, per_device(): pl.pallas_call(functools.partial(kernel, nx, ny, 1.0 / math.sqrt(cells)),...  33.6 us
    unnamed x1, local copies, waits for them, and re-layouts  1.4 us

profile of v5, /device:TPU:0, one launch (start us, length us, event | category | flops | bytes accessed | tf_op | source)
XLA Modules:
  0.0 36.3 jit_solution(14287241098861059741)
XLA Ops:
  0.6 33.6 %shard_map.68 = (f32[9,512,128]{2,1,0:T(8,128)S(1)}, f32[16,128]{1,0:T(8,128)S(1)}) custom-call(f32[9,512,128]{2,1,0:T(8,128)} %bitcast.7, s32[512,128]{1,0:T(8,128)} %bitcast.8, s32[512,128]{1,0:T(8,128)} %bitcast.9, s32[512,128]{1,0:T(8,128)} %bitcast.10, s32[512,128]{1,0:T(8,128)} %bitcast.11), custom_call_target="tpu_custom_call" | custom-call | tf_op jit(solution)/shard_map/pallas_call | solution.py:798
  34.3 0.6 %slice_reduce_fusion = f32[9]{0:T(128)} fusion(f32[16,128]{1,0:T(8,128)S(1)} %get-tuple-element.5), kind=kLoop, calls=%fused_computation | loop fusion | bytes 72 | tf_op jit(solution)/shard_map/slice | solution.py:821
  34.9 1.4 %copy.8 = f32[9,32,16,128]{3,2,1,0:T(8,128)} copy(f32[9,32,16,128]{3,2,1,0:T(8,128)S(1)} %bitcast.6) | data formatting | bytes 4718592

commit v6 on v5

--- a/solution.py
+++ b/solution.py
@@ -50,7 +50,7 @@
     codes, wbuf, qbuf, packed, shifted, edge,
     zl_i, zr_i, zs_f, zl_f, zr_f,
     ys_i, yr_i, cs_i, cr_i, ys_p, yr_p, cs_p, cr_p,
-    xr_r, ys_r, yr_r, cs_r, cr_r, xr_w, ys_w, yr_w, cs_w, cr_w, xr_q, ys_q, yr_q, cs_q, cr_q,
+    xr_r, ys_r, yr_r, cs_r, cr_r, xr_w, ys_w, yr_w, cs_w, cr_w, xr_q, ys_q, yr_q, cs_q, cr_q, xs_q,
     volumes, weights, gathered, scaling, parts_i, parts_f, parts_e, peers,
     load, z_send, z_recv, send, recv, peer_send, peer_recv,
 ):
@@ -263,14 +263,17 @@
             pl.when(below_z)(self.copies[1].wait_send)
 
     class Faces:
-        def __init__(self, number, buf, n, start, step, landing):
-            self.buf, self.n, self.first_row, self.step = buf, n, start, step
+        def __init__(self, number, buf, n, start, step, landing, xs=None):
+            self.buf, self.n, self.first_row, self.step, self.xs = buf, n, start, step, xs
             self.xr, self.ys, self.yr, self.cs, self.cr = landing
             self.copies = []
             for k, (dx, dy) in enumerate(WAYS):
                 way = 0 if dx + dy > 0 else 1
                 if dy == 0:
-                    source = buf.at[pl.ds(0, n), pl.ds(start + (nx - 1 if dx > 0 else 0) * step, ny), :]
+                    if xs is None:
+                        source = buf.at[pl.ds(0, n), pl.ds(start + (nx - 1 if dx > 0 else 0) * step, ny), :]
+                    else:
+                        source = xs.at[way]
                     target = self.xr.at[way, pl.ds(0, n), pl.ds(TILE, ny), :]
                 elif dx == 0:
                     source, target = self.ys.at[way], self.yr.at[way, pl.ds(0, n), pl.ds(TILE, nx), :]
@@ -326,6 +329,18 @@
             for k in range(2, 8):
                 pl.when(exists(*WAYS[k]))(self.copies[k].start)
 
+        def start_filled(self):
+            def corners(f, carry):
+                for k, (dx, dy) in enumerate(WAYS[4:]):
+                    self.cs[k, pl.ds(f, 1), :] = self.xs[0 if dx > 0 else 1, f, pl.ds(edge_row(dy), 1), :]
+                return carry
+
+            for k in range(4):
+                pl.when(exists(*WAYS[k]))(self.copies[k].start)
+            lax.fori_loop(0, self.n, corners, 0)
+            for k in range(4, 8):
+                pl.when(exists(*WAYS[k]))(self.copies[k].start)
+
         def receive(self):
             for k, (dx, dy) in enumerate(WAYS):
                 pl.when(exists(-dx, -dy))(self.copies[k].wait_recv)
@@ -369,7 +384,7 @@
     w_all = Faces(4, weights, 1, 0, ny, (xr_w, ys_w, yr_w, cs_w, cr_w))
     w_packed = Unit(5, packed, 1, 2, ys_p, yr_p, cs_p, cr_p, 1)
     q_z = Depth(3, zs_f.at[2], zl_f.at[2], zr_f.at[2], packed, 2)
-    q_all = Faces(6, qbuf, nspec, first(1), pitch, (xr_q, ys_q, yr_q, cs_q, cr_q))
+    q_all = Faces(6, qbuf, nspec, first(1), pitch, (xr_q, ys_q, yr_q, cs_q, cr_q), xs_q)
     q_packed = Unit(7, packed, 2, 3, ys_p, yr_p, cs_p, cr_p, 2)
     everything = [
         code_z, code_own, code_packed, raw_z, raw_all, raw_packed, w_z, w_all, w_packed, q_z, q_all, q_packed,
@@ -471,8 +486,9 @@
     def packed_taps(row, step, source, value_of):
         zero = jnp.zeros((TILE, LANES), jnp.float32)
         total = None
+        row = row - (pitch + TILE)
         for a, b, position in BLOCK:
-            near = pl.ds(row + step * (a * pitch + b), TILE)
+            near = pl.ds(row + (pitch + TILE + step * (a * pitch + b)), TILE)
             term = jnp.where((source(near) & (1 << position)) != 0, value_of(near), zero)
             total = term if total is None else total + term
         return total
@@ -484,7 +500,7 @@
             packed = jnp.where((lane == 2 * f) | (lane == 2 * f + 1), pltpu.roll(value, 2 * f + 1, 1), packed)
         return packed
 
-    quad = 2
+    quad = 4
     members = [(k, k // tiles, k % tiles) for k in range(quad * tiles)]
 
     def count_taps(g):
@@ -492,8 +508,9 @@
             row, at = own_tile(g * quad + x, y)
             sums = [None] * 3
             total = None
+            row = row - (pitch + TILE)
             for a, b, position in BLOCK:
-                near = pl.ds(row - a * pitch - b, TILE)
+                near = pl.ds(row + (pitch + TILE - a * pitch - b), TILE)
                 value = codes[0, near, :]
                 value = value if position == 0 else lax.shift_right_logical(value, position)
                 for m in range(3):
@@ -550,9 +567,11 @@
         own = pl.ds(at, TILE)
         right, left, middle = shifted[0, own, :], shifted[1, own, :], codes[0, pl.ds(row, TILE), :]
         taps = []
+        base = row - (pitch + TILE)
         for a, b, position in BLOCK:
             center = None if position == 12 else middle
-            taps.append(((left, center, right), position, reader(wbuf, pl.ds(row + a * pitch + b, TILE))))
+            near = pl.ds(base + (pitch + TILE + a * pitch + b), TILE)
+            taps.append(((left, center, right), position, reader(wbuf, near)))
         keep_sums(0, masked_sums(taps, 0, fields), 0)
 
     def gather_close(t):
@@ -603,6 +622,41 @@
             own = pl.ds(at, TILE)
             gathered[own, :] = gathered[own, :] + merged(way * tiles + k, flux, False)
 
+    def edge_tiles():
+        for way, y in enumerate((ny - 1, 0)):
+            for x in range(0, nx, TILE):
+                row = first(x + 1) + y
+                yield (
+                    lambda start: pl.ds(start, TILE, stride=pitch), row,
+                    pl.ds(x * ny + y, TILE, stride=ny), ys_q.at[way], pl.ds(x, TILE),
+                )
+        for way, x in enumerate((nx - 1, 0)):
+            for k in range(tiles):
+                row, at = own_tile(x, k)
+                yield lambda start: pl.ds(start, TILE), row, pl.ds(at, TILE), xs_q.at[way], pl.ds(k * TILE, TILE)
+
+    def edge_ends():
+        zero = jnp.zeros((TILE, LANES), jnp.float32)
+        for n, (rows, row, own, _, _) in enumerate(edge_tiles()):
+            bits = edge[own, :]
+            total = None
+            for a, b, position in BLOCK:
+                near = rows(row + a * pitch + b)
+                term = jnp.where((bits & (1 << position)) != 0, packed[0, near, :] * packed[1, near, :], zero)
+                total = term if total is None else total + term
+            parts_e[n] = total
+
+    def edge_quotas():
+        for n, (rows, row, own, ref, where) in enumerate(edge_tiles()):
+            value = parts_e[n]
+
+            def spread(f):
+                return jnp.where(both_ends, pltpu.roll(value, LANES - 1 - 2 * f, 1), 0.0)
+
+            inverted = 1.0 / (gathered[own, :] + spread(flux))
+            for f in range(nspec):
+                ref[f, where, :] = (qbuf[f, rows(row), :] + spread(f)) * inverted
+
     def gather_ends(g):
         for k, x, y in members:
             row, at = own_tile(g * quad + x, y)
@@ -629,9 +683,10 @@
 
     def scatter_main(t):
         row, at = own_tile(t // tiles, t % tiles) if isinstance(t, int) else own_row(t)
+        row = row - (pitch + TILE)
         taps = []
         for a, b, position in BLOCK:
-            near = pl.ds(row - a * pitch - b, TILE)
+            near = pl.ds(row + (pitch + TILE - a * pitch - b), TILE)
             source = codes[0, near, :]
             center = None if position == 12 else source
             taps.append(((source, center, source), position, reader(qbuf, near)))
@@ -738,16 +793,18 @@
     for stage in (gather_plane, gather_plane_close):
         stage(0)
         stage(1)
+    edge_ends()
+    edge_quotas()
+    q_all.start_filled()
     pipelined([gather_ends, quotas, quota_pack], nx // quad)
     q_z.start()
-    q_all.start()
 
     def relay_q():
         q_z.receive()
         q_packed.start()
         next(reduction)
 
-    pipelined([scatter_main, scatter_close], nx * tiles, (nx * tiles // 4, relay_q))
+    pipelined([scatter_main, scatter_close], nx * tiles, (nx * tiles // 5, relay_q))
     q_all.receive()
     q_packed.receive()
     next(reduction)
@@ -757,8 +814,17 @@
         stage(1)
     pipelined([scatter_ends, finals], nx // quad)
     next(reduction, None)
-    for part in everything:
-        part.finish()
+    flat = [part for part in everything if not isinstance(part, Depth)]
+    deep = [part for part in everything if isinstance(part, Depth)]
+
+    def drain(copies):
+        for copy in copies:
+            copy.wait_send()
+
+    for k, (dx, dy) in enumerate(WAYS):
+        pl.when(exists(dx, dy))(functools.partial(drain, [part.copies[k] for part in flat]))
+    pl.when(above_z)(functools.partial(drain, [part.copies[0] for part in deep]))
+    pl.when(below_z)(functools.partial(drain, [part.copies[1] for part in deep]))
 
 
 def per_device(provisional, cut_flag, cut_code, volume_level, area_level):
@@ -790,8 +856,8 @@
         ]
     high = -(-nspec // TILE) * TILE
     shapes += [
-        ((own, nz), f32), ((1, own, nz), f32), ((own, nz), f32), ((own, nz), f32),
-        ((2 * tiles, 4, TILE, nz), i32), ((2 * tiles, 3, fields, TILE, nz), f32), ((2 * tiles, TILE, nz), f32),
+        ((2, nspec, ny, nz), f32), ((own, nz), f32), ((1, own, nz), f32), ((own, nz), f32), ((own, nz), f32),
+        ((4 * tiles, 4, TILE, nz), i32), ((2 * tiles, 3, fields, TILE, nz), f32), ((max(4 * tiles, 2 * (tiles + nx // TILE)), TILE, nz), f32),
         ((3, most, high, nz), f32),
     ]
     dma = pltpu.SemaphoreType.DMA

time: 36.5 us -> 33.9 us (0.929)
  Pallas kernels: 33.6 us -> 31.1 us
    pallas_call x1, Pallas kernels: 33.6 us -> 31.1 us  [per_device(): pl.pallas_call(functools.partial(kernel, nx, ny, 1.0 / math.sqrt(cells)),...]
where the time goes in v6:
time: 33.9 us; the launch traced here: 33.7 us
  Pallas kernels  31.1 us (92%)
  local copies, waits for them, and re-layouts  2.03 us (6%)
  between operations  0.64 us (2%)
    pallas_call x1, Pallas kernels, per_device(): pl.pallas_call(functools.partial(kernel, nx, ny, 1.0 / math.sqrt(cells)),...  31.1 us
    unnamed x1, local copies, waits for them, and re-layouts  1.4 us

profile of v6, /device:TPU:0, one launch (start us, length us, event | category | flops | bytes accessed | tf_op | source)
XLA Modules:
  0.0 33.7 jit_solution(17010305196667250135)
XLA Ops:
  0.6 31.1 %shard_map.68 = (f32[9,512,128]{2,1,0:T(8,128)S(1)}, f32[16,128]{1,0:T(8,128)S(1)}) custom-call(f32[9,512,128]{2,1,0:T(8,128)} %bitcast.7, s32[512,128]{1,0:T(8,128)} %bitcast.8, s32[512,128]{1,0:T(8,128)} %bitcast.9, s32[512,128]{1,0:T(8,128)} %bitcast.10, s32[512,128]{1,0:T(8,128)} %bitcast.11), custom_call_target="tpu_custom_call" | custom-call | tf_op jit(solution)/shard_map/pallas_call | solution.py:864
  31.7 0.6 %slice_reduce_fusion = f32[9]{0:T(128)} fusion(f32[16,128]{1,0:T(8,128)S(1)} %get-tuple-element.5), kind=kLoop, calls=%fused_computation | loop fusion | bytes 72 | tf_op jit(solution)/shard_map/slice | solution.py:887
  32.3 1.4 %copy.8 = f32[9,32,16,128]{3,2,1,0:T(8,128)} copy(f32[9,32,16,128]{3,2,1,0:T(8,128)S(1)} %bitcast.6) | data formatting | bytes 4718592

commit v7 on v6

--- a/solution.py
+++ b/solution.py
@@ -50,7 +50,7 @@
     codes, wbuf, qbuf, packed, shifted, edge,
     zl_i, zr_i, zs_f, zl_f, zr_f,
     ys_i, yr_i, cs_i, cr_i, ys_p, yr_p, cs_p, cr_p,
-    xr_r, ys_r, yr_r, cs_r, cr_r, xr_w, ys_w, yr_w, cs_w, cr_w, xr_q, ys_q, yr_q, cs_q, cr_q, xs_q,
+    xr_r, ys_r, yr_r, cs_r, cr_r, xr_w, ys_w, yr_w, cs_w, cr_w, xr_q, ys_q, yr_q, cs_q, cr_q, xs_q, xr_c, ys_c, yr_c, cs_c, cr_c,
     volumes, weights, gathered, scaling, parts_i, parts_f, parts_e, peers,
     load, z_send, z_recv, send, recv, peer_send, peer_recv,
 ):
@@ -79,7 +79,7 @@
     near_x = lax.min(here["gx"], 1) + lax.min(size["gx"] - 1 - here["gx"], 1)
     near_y = lax.min(here["gy"], 1) + lax.min(size["gy"] - 1 - here["gy"], 1)
     near_z = lax.min(here["gz"], 1) + lax.min(size["gz"] - 1 - here["gz"], 1)
-    greeted = (near_x + 1) * (near_y + 1) - 1 + near_z
+    greeted = (near_x + 1) * (near_y + 1) * (near_z + 1) - 1
     for axis, near in (("gx", near_x), ("gy", near_y), ("gz", near_z)):
         if size[axis] > 4:
             greeted = greeted + (size[axis] - 1 - near)
@@ -110,7 +110,11 @@
 
     below_z, above_z = side("gz", -1), side("gz", 1)
     for dx, dy in WAYS:
-        pl.when(exists(dx, dy))(functools.partial(greet, {"gx": moved("gx", dx), "gy": moved("gy", dy)}))
+        around = {"gx": moved("gx", dx), "gy": moved("gy", dy)}
+        pl.when(exists(dx, dy))(functools.partial(greet, around))
+        for dz in (-1, 1):
+            there = jnp.logical_and(exists(dx, dy), above_z if dz > 0 else below_z)
+            pl.when(there)(functools.partial(greet, {**around, "gz": moved("gz", dz)}))
     pl.when(below_z)(functools.partial(greet, {"gz": moved("gz", -1)}))
     pl.when(above_z)(functools.partial(greet, {"gz": moved("gz", 1)}))
     for axis in AXES:
@@ -263,7 +267,8 @@
             pl.when(below_z)(self.copies[1].wait_send)
 
     class Faces:
-        def __init__(self, number, buf, n, start, step, landing, xs=None):
+        def __init__(self, number, buf, n, start, step, landing, xs=None, dz=0):
+            self.dz = dz
             self.buf, self.n, self.first_row, self.step, self.xs = buf, n, start, step, xs
             self.xr, self.ys, self.yr, self.cs, self.cr = landing
             self.copies = []
@@ -283,9 +288,23 @@
                     pltpu.make_async_remote_copy(
                         src_ref=source, dst_ref=target,
                         send_sem=send.at[number, k], recv_sem=recv.at[number, k],
-                        device_id={"gx": moved("gx", dx), "gy": moved("gy", dy)}, device_id_type=MESH,
+                        device_id={"gx": moved("gx", dx), "gy": moved("gy", dy), "gz": moved("gz", dz)}, device_id_type=MESH,
                     )
                 )
+
+        def there(self, dx, dy):
+            if self.dz == 0:
+                return exists(dx, dy)
+            return jnp.logical_and(exists(dx, dy), above_z if self.dz > 0 else below_z)
+
+        def incoming(self, dx, dy):
+            if self.dz == 0:
+                return exists(-dx, -dy)
+            return jnp.logical_and(exists(-dx, -dy), below_z if self.dz > 0 else above_z)
+
+        def land(self):
+            for k, (dx, dy) in enumerate(WAYS):
+                pl.when(self.incoming(dx, dy))(self.copies[k].wait_recv)
 
         def blank(self):
             zeros = jnp.zeros((TILE, LANES), jnp.float32)
@@ -310,7 +329,7 @@
                 pl.when(jnp.logical_not(exists(-step, 0)))(functools.partial(clear, self.xr, way, ny))
                 pl.when(jnp.logical_not(exists(0, -step)))(functools.partial(clear, self.yr, way, nx))
 
-        def start(self):
+        def collect(self):
             buf, step = self.buf, self.step
 
             def gather(f, carry):
@@ -323,11 +342,11 @@
                     self.cs[k, pl.ds(f, 1), :] = buf[f, pl.ds(row, 1), :]
                 return carry
 
-            for k in range(2):
-                pl.when(exists(*WAYS[k]))(self.copies[k].start)
             lax.fori_loop(0, self.n, gather, 0)
-            for k in range(2, 8):
-                pl.when(exists(*WAYS[k]))(self.copies[k].start)
+
+        def launch(self):
+            for k in range(8):
+                pl.when(self.there(*WAYS[k]))(self.copies[k].start)
 
         def start_filled(self):
             def corners(f, carry):
@@ -359,7 +378,7 @@
 
         def finish(self):
             for k, (dx, dy) in enumerate(WAYS):
-                pl.when(exists(dx, dy))(self.copies[k].wait_send)
+                pl.when(self.there(dx, dy))(self.copies[k].wait_send)
 
     def pad_zeros(buf, n):
         zeros = jnp.zeros((TILE, LANES), jnp.float32)
@@ -374,9 +393,10 @@
 
         lax.fori_loop(0, n, body, 0)
 
-    code_z = Depth(0, edge, zl_i, zr_i, codes, 1)
+    code_z = Depth(0, edge.at[0], zl_i, zr_i, codes, 1)
     code_own = Unit(0, codes, 0, 1, ys_i, yr_i, cs_i, cr_i, 0)
-    code_packed = Unit(1, codes, 1, 2, ys_i, yr_i, cs_i, cr_i, 1)
+    code_up = Faces(1, edge, 1, 0, ny, (xr_c.at[0], ys_c, yr_c.at[0], cs_c, cr_c.at[0]), None, 1)
+    code_down = Faces(8, edge, 1, 0, ny, (xr_c.at[1], ys_c, yr_c.at[1], cs_c, cr_c.at[1]), None, -1)
     raw_z = Depth(1, zs_f.at[0], zl_f.at[0], zr_f.at[0], packed, 0)
     raw_all = Faces(2, raw, fields, 0, ny, (xr_r, ys_r, yr_r, cs_r, cr_r))
     raw_packed = Unit(3, packed, 0, 1, ys_p, yr_p, cs_p, cr_p, 0)
@@ -387,8 +407,40 @@
     q_all = Faces(6, qbuf, nspec, first(1), pitch, (xr_q, ys_q, yr_q, cs_q, cr_q), xs_q)
     q_packed = Unit(7, packed, 2, 3, ys_p, yr_p, cs_p, cr_p, 2)
     everything = [
-        code_z, code_own, code_packed, raw_z, raw_all, raw_packed, w_z, w_all, w_packed, q_z, q_all, q_packed,
+        code_z, code_own, raw_z, raw_all, raw_packed, w_z, w_all, w_packed, q_z, q_all, q_packed,
     ]
+
+    def join_code_ends():
+        code_up.land()
+        code_down.land()
+        zero = jnp.zeros((TILE, LANES), jnp.int32)
+
+        def mixed(low, high):
+            low = jnp.where(below_z, pltpu.roll(low, 1, 1), zero)
+            high = jnp.where(above_z, pltpu.roll(high, LANES - 1, 1), zero)
+            return jnp.where(odd, low, high)
+
+        def plane(way, step):
+            for k in range(tiles):
+                near = pl.ds(TILE + k * TILE, TILE)
+                row = first(0 if step > 0 else nx + 1) + k * TILE
+                codes[1, pl.ds(row, TILE), :] = mixed(xr_c[0, way, 0, near, :], xr_c[1, way, 0, near, :])
+
+        def rows(way, step):
+            for x in range(0, nx, TILE):
+                near = pl.ds(TILE + x, TILE)
+                row = first(x + 1) + halo_row(-step)
+                codes[1, pl.ds(row, TILE, stride=pitch), :] = mixed(yr_c[0, way, 0, near, :], yr_c[1, way, 0, near, :])
+
+        def corner(k, dx, dy):
+            row = first(0 if dx > 0 else nx + 1) + halo_row(-dy)
+            codes[1, pl.ds(row, 1), :] = mixed(cr_c[0, k], cr_c[1, k])[:1]
+
+        for way, step in ((0, 1), (1, -1)):
+            pl.when(exists(-step, 0))(functools.partial(plane, way, step))
+            pl.when(exists(0, -step))(functools.partial(rows, way, step))
+        for k, (dx, dy) in enumerate(WAYS[4:]):
+            pl.when(exists(-dx, -dy))(functools.partial(corner, k, dx, dy))
 
     def total_over(value):
         for number, axis in enumerate(AXES):
@@ -410,7 +462,9 @@
             value = peers[number, 0]
             for k in range(1, n):
                 value = value + peers[number, k]
-        change[...] = jnp.broadcast_to(jnp.sum(value, axis=1, keepdims=True) * scale, change.shape)
+        sums = jnp.broadcast_to(jnp.sum(value, axis=1, keepdims=True) * scale, value.shape)
+        places = lax.broadcasted_iota(jnp.int32, value.shape, 1) == lax.broadcasted_iota(jnp.int32, value.shape, 0)
+        change[...] = jnp.sum(jnp.where(places, sums, 0.0), axis=0)[:nspec]
 
     def fractions(own):
         is_cut = flag[own, :] == 1
@@ -426,7 +480,7 @@
             codes[0, pl.ds(row, TILE), :] = value
             low = jnp.broadcast_to(value[:, :1], (TILE, LANES))
             high = lax.shift_right_logical(jnp.broadcast_to(value[:, LANES - 1:], (TILE, LANES)), 2)
-            edge[own, :] = jnp.where(odd, low, high)
+            edge[0, own, :] = jnp.where(odd, low, high)
         return carry
 
     def shift(x, carry):
@@ -638,7 +692,7 @@
     def edge_ends():
         zero = jnp.zeros((TILE, LANES), jnp.float32)
         for n, (rows, row, own, _, _) in enumerate(edge_tiles()):
-            bits = edge[own, :]
+            bits = edge[0, own, :]
             total = None
             for a, b, position in BLOCK:
                 near = rows(row + a * pitch + b)
@@ -660,7 +714,7 @@
     def gather_ends(g):
         for k, x, y in members:
             row, at = own_tile(g * quad + x, y)
-            value = edge[pl.ds(at, TILE), :]
+            value = edge[0, pl.ds(at, TILE), :]
             parts_e[k] = packed_taps(
                 row, 1, lambda near: value, lambda near: packed[0, near, :] * packed[1, near, :])
 
@@ -749,6 +803,9 @@
     pl.semaphore_wait(barrier, greeted)
     code_z.start()
     code_own.start()
+    code_up.collect()
+    code_up.launch()
+    code_down.launch()
     for copy in loads[2:]:
         copy.wait()
     totals = tuple(jnp.zeros((TILE, LANES), jnp.float32) for _ in range(nspec))
@@ -759,9 +816,8 @@
         axis=0,
     )
     reduction = total_over(local)
-    code_z.receive()
-    code_packed.start()
-    raw_all.start()
+    raw_all.collect()
+    raw_all.launch()
     lax.fori_loop(0, nx, raw_pack, 0, unroll=4)
     raw_z.start()
     lax.fori_loop(0, nx, shift, 0, unroll=8)
@@ -771,13 +827,15 @@
     q_all.blank()
     pad_zeros(wbuf, fields)
     pad_zeros(qbuf, nspec)
-    code_own.receive()
-    code_packed.receive()
     raw_z.receive()
     raw_packed.start()
+    code_z.receive()
+    code_own.receive()
+    join_code_ends()
     pipelined([count_taps, weigh, weigh_pack], nx // quad)
     w_z.start()
-    w_all.start()
+    w_all.collect()
+    w_all.launch()
 
     def relay_w():
         w_z.receive()
@@ -785,14 +843,14 @@
 
     pipelined([gather_main, gather_close], nx * tiles, (nx * tiles // 4, relay_w))
     raw_all.receive()
-    raw_packed.receive()
     w_all.receive()
-    w_packed.receive()
     next(reduction)
     pipelined([gather_strip, gather_strip_close], nx // TILE)
     for stage in (gather_plane, gather_plane_close):
         stage(0)
         stage(1)
+    raw_packed.receive()
+    w_packed.receive()
     edge_ends()
     edge_quotas()
     q_all.start_filled()
@@ -806,12 +864,12 @@
 
     pipelined([scatter_main, scatter_close], nx * tiles, (nx * tiles // 5, relay_q))
     q_all.receive()
-    q_packed.receive()
     next(reduction)
     pipelined([scatter_strip, scatter_strip_close], nx // TILE)
     for stage in (scatter_plane, scatter_plane_close):
         stage(0)
         stage(1)
+    q_packed.receive()
     pipelined([scatter_ends, finals], nx // quad)
     next(reduction, None)
     flat = [part for part in everything if not isinstance(part, Depth)]
@@ -823,6 +881,8 @@
 
     for k, (dx, dy) in enumerate(WAYS):
         pl.when(exists(dx, dy))(functools.partial(drain, [part.copies[k] for part in flat]))
+    code_up.finish()
+    code_down.finish()
     pl.when(above_z)(functools.partial(drain, [part.copies[0] for part in deep]))
     pl.when(below_z)(functools.partial(drain, [part.copies[1] for part in deep]))
 
@@ -842,7 +902,7 @@
     shapes = [
         ((fields, own, nz), f32), ((own, nz), i32), ((own, nz), i32), ((own, nz), i32), ((own, nz), i32),
         ((2, rows, nz), i32), ((fields, rows, nz), f32), ((nspec, rows, nz), f32), ((3, rows, nz), f32),
-        ((2, own, nz), i32), ((own, nz), i32),
+        ((2, own, nz), i32), ((1, own, nz), i32),
         ((own, nz), i32), ((own, nz), i32),
         ((3, own, nz), f32), ((3, own, nz), f32), ((3, own, nz), f32),
         ((2, 2, nx, nz), i32), ((2, 2, nx, nz), i32), ((2, 4, TILE, nz), i32), ((2, 4, TILE, nz), i32),
@@ -856,7 +916,10 @@
         ]
     high = -(-nspec // TILE) * TILE
     shapes += [
-        ((2, nspec, ny, nz), f32), ((own, nz), f32), ((1, own, nz), f32), ((own, nz), f32), ((own, nz), f32),
+        ((2, nspec, ny, nz), f32),
+        ((2, 2, 1, ny + 2 * TILE, nz), i32), ((2, 1, nx, nz), i32), ((2, 2, 1, nx + 2 * TILE, nz), i32),
+        ((4, TILE, nz), i32), ((2, 4, TILE, nz), i32),
+        ((own, nz), f32), ((1, own, nz), f32), ((own, nz), f32), ((own, nz), f32),
         ((4 * tiles, 4, TILE, nz), i32), ((2 * tiles, 3, fields, TILE, nz), f32), ((max(4 * tiles, 2 * (tiles + nx // TILE)), TILE, nz), f32),
         ((3, most, high, nz), f32),
     ]
@@ -865,13 +928,13 @@
         functools.partial(kernel, nx, ny, 1.0 / math.sqrt(cells)),
         out_shape=(
             jax.ShapeDtypeStruct((nspec, own, nz), f32),
-            jax.ShapeDtypeStruct((high, nz), f32),
+            jax.ShapeDtypeStruct((nspec,), f32),
         ),
         in_specs=[hbm] * 5,
         out_specs=(vmem, vmem),
         scratch_shapes=[pltpu.VMEM(shape, kind) for shape, kind in shapes]
         + [
-            dma((5,)), dma((4, 2)), dma((4, 2)), dma((8, 8)), dma((8, 8)), dma((3, most)), dma((3, most)),
+            dma((5,)), dma((4, 2)), dma((4, 2)), dma((9, 8)), dma((9, 8)), dma((3, most)), dma((3, most)),
         ],
         compiler_params=pltpu.CompilerParams(
             collective_id=0, has_side_effects=True, vmem_limit_bytes=26 * 1024 * 1024
@@ -884,7 +947,7 @@
         volume_level.reshape(own, nz),
         area_level.reshape(own, nz))]
     )
-    return out.reshape(provisional.shape), change[:nspec, 0]
+    return out.reshape(provisional.shape), change
 
 
 def solution(mesh):

time: 33.9 us -> 33.1 us (0.976)
  Pallas kernels: 31.1 us -> 30.4 us
    pallas_call x1, Pallas kernels: 31.1 us -> 30.4 us  [per_device(): pl.pallas_call(functools.partial(kernel, nx, ny, 1.0 / math.sqrt(cells)),...]
    slice x1 -> x0, local copies, waits for them, and re-layouts: 0.63 us -> none  [per_device(): return (out.reshape(provisional.shape), change[:nspec, 0])]
    unnamed x1 -> x2, local copies, waits for them, and re-layouts: 1.4 us -> 1.92 us
where the time goes in v7:
time: 33.1 us; the launch traced here: 33 us
  Pallas kernels  30.4 us (92%)
  local copies, waits for them, and re-layouts  1.92 us (6%)
  between operations  0.64 us (2%)
    pallas_call x1, Pallas kernels, per_device(): pl.pallas_call(functools.partial(kernel, nx, ny, 1.0 / math.sqrt(cells)),...  30.4 us
    unnamed x2, local copies, waits for them, and re-layouts  1.92 us

profile of v7, /device:TPU:0, one launch (start us, length us, event | category | flops | bytes accessed | tf_op | source)
XLA Modules:
  0.0 33.0 jit_solution(16941623550956636812)
XLA Ops:
  0.6 30.4 %shard_map.68 = (f32[9,512,128]{2,1,0:T(8,128)S(1)}, f32[9]{0:T(128)S(1)}) custom-call(f32[9,512,128]{2,1,0:T(8,128)} %bitcast.7, s32[512,128]{1,0:T(8,128)} %bitcast.8, s32[512,128]{1,0:T(8,128)} %bitcast.9, s32[512,128]{1,0:T(8,128)} %bitcast.10, s32[512,128]{1,0:T(8,128)} %bitcast.11), custom_call_target="tpu_custom_call" | custom-call | tf_op jit(solution)/shard_map/pallas_call | solution.py:927
  31.1 1.4 %copy.9 = f32[9,32,16,128]{3,2,1,0:T(8,128)} copy(f32[9,32,16,128]{3,2,1,0:T(8,128)S(1)} %bitcast.6) | data formatting | bytes 4718592
  32.5 0.5 %copy.10 = f32[9]{0:T(128)} copy(f32[9]{0:T(128)S(1)} %get-tuple-element.9) | data formatting | bytes 72

commit v8 on v7

--- a/solution.py
+++ b/solution.py
@@ -185,10 +185,6 @@
 
         def start(self):
             buf = self.buf
-            for k, (dx, dy) in enumerate(WAYS):
-                if dy == 0:
-                    pl.when(exists(dx, dy))(self.copies[k].start)
-
             def gather(f, carry):
                 for x in range(0, nx, TILE):
                     for way, step in ((0, 1), (1, -1)):
@@ -199,9 +195,8 @@
                 return carry
 
             lax.fori_loop(self.low, self.high, gather, 0)
-            for k, (dx, dy) in enumerate(WAYS):
-                if dy != 0:
-                    pl.when(exists(dx, dy))(self.copies[k].start)
+            for k in (4, 5, 6, 7, 0, 1, 2, 3):
+                pl.when(exists(*WAYS[k]))(self.copies[k].start)
 
         def receive(self):
             buf = self.buf
@@ -345,7 +340,7 @@
             lax.fori_loop(0, self.n, gather, 0)
 
         def launch(self):
-            for k in range(8):
+            for k in (4, 5, 6, 7, 0, 1, 2, 3):
                 pl.when(self.there(*WAYS[k]))(self.copies[k].start)
 
         def start_filled(self):
@@ -354,10 +349,8 @@
                     self.cs[k, pl.ds(f, 1), :] = self.xs[0 if dx > 0 else 1, f, pl.ds(edge_row(dy), 1), :]
                 return carry
 
-            for k in range(4):
-                pl.when(exists(*WAYS[k]))(self.copies[k].start)
             lax.fori_loop(0, self.n, corners, 0)
-            for k in range(4, 8):
+            for k in (4, 5, 6, 7, 0, 1, 2, 3):
                 pl.when(exists(*WAYS[k]))(self.copies[k].start)
 
         def receive(self):

time: 33.1 us -> 32.8 us (level)
  no operation moved by 1% of the time
where the time goes in v8:
time: 32.8 us; the launch traced here: 32.6 us
  Pallas kernels  30.1 us (92%)
  local copies, waits for them, and re-layouts  1.92 us (6%)
  between operations  0.64 us (2%)
    pallas_call x1, Pallas kernels, per_device(): pl.pallas_call(functools.partial(kernel, nx, ny, 1.0 / math.sqrt(cells)),...  30.1 us
    unnamed x2, local copies, waits for them, and re-layouts  1.92 us

profile of v8, /device:TPU:0, one launch (start us, length us, event | category | flops | bytes accessed | tf_op | source)
XLA Modules:
  0.0 32.6 jit_solution(7977167233441641537)
XLA Ops:
  0.6 30.1 %shard_map.68 = (f32[9,512,128]{2,1,0:T(8,128)S(1)}, f32[9]{0:T(128)S(1)}) custom-call(f32[9,512,128]{2,1,0:T(8,128)} %bitcast.7, s32[512,128]{1,0:T(8,128)} %bitcast.8, s32[512,128]{1,0:T(8,128)} %bitcast.9, s32[512,128]{1,0:T(8,128)} %bitcast.10, s32[512,128]{1,0:T(8,128)} %bitcast.11), custom_call_target="tpu_custom_call" | custom-call | tf_op jit(solution)/shard_map/pallas_call | solution.py:920
  30.7 1.4 %copy.9 = f32[9,32,16,128]{3,2,1,0:T(8,128)} copy(f32[9,32,16,128]{3,2,1,0:T(8,128)S(1)} %bitcast.6) | data formatting | bytes 4718592
  32.1 0.5 %copy.10 = f32[9]{0:T(128)} copy(f32[9]{0:T(128)S(1)} %get-tuple-element.9) | data formatting | bytes 72
